TPU v7x, 128 devices: a whole 4x4x4 slice. The times are simulated.
128 devices in a mesh: rep: 1, tp: 16 (over z, y), dp: 8 (over x, core).
Axes of the slice: x: 4, y: 4, z: 4, core: 2. Of those that a mesh axis runs over, the one named last changes fastest.
Arguments:
- grad_partial: float32 [8, 8, 1024, 2048], P(('rep', 'dp'), None, None, 'tp')
- momentum: float32 [8, 1024, 2048], P('rep', 'dp', 'tp')
- weight: float32 [8, 1024, 2048], P('rep', 'dp', 'tp')
- learn_rate: float32 [8], P('rep')
- decay_rate: float32 [], replicated
Outputs:
- output 1: float32 [8, 1024, 2048], P('rep', 'dp', 'tp')
- output 2: float32 [8, 1024, 2048], P('rep', 'dp', 'tp')
- output 3: bfloat16 [8, 1024, 2048], P('rep', None, 'tp')
All inputs are finite; a program needn't handle non-finite values.
Results may differ from a plain program's by a relative error of at most 0.0131549.
Values are sent between devices in bfloat16 or wider.
A program may use at most 1 GiB of HBM per device.

v0:
```python
import math
import jax
import jax.numpy as jnp
from jax import lax
from jax.sharding import PartitionSpec as P, NamedSharding

MOMENTUM = 0.95
NS_STEPS = 5
COEF_A = 3.4445
COEF_B = -4.7750
COEF_C = 2.0315
NORM_EPS = 1e-7


def newton_schulz(update, short_rows):
    upd_f32 = update.astype(jnp.float32)
    norm_val = jnp.sqrt(jnp.sum(upd_f32 * upd_f32, axis=(1, 2), keepdims=True))
    x_cur = (upd_f32 / (norm_val + NORM_EPS)).astype(jnp.bfloat16)
    for step_idx in range(NS_STEPS):
        if short_rows:
            gram_mat = jnp.einsum("bik,bjk->bij", x_cur, x_cur, preferred_element_type=jnp.float32)
        else:
            gram_mat = jnp.einsum("bki,bkj->bij", x_cur, x_cur, preferred_element_type=jnp.float32)
        gram_mat = gram_mat.astype(jnp.bfloat16)
        gram_sq = jnp.einsum("bij,bjk->bik", gram_mat, gram_mat, preferred_element_type=jnp.float32)
        poly_mat = (COEF_B * gram_mat.astype(jnp.float32) + COEF_C * gram_sq).astype(jnp.bfloat16)
        if short_rows:
            prod_mat = jnp.einsum("bij,bjk->bik", poly_mat, x_cur, preferred_element_type=jnp.float32)
        else:
            prod_mat = jnp.einsum("bkj,bij->bki", x_cur, poly_mat, preferred_element_type=jnp.float32)
        x_cur = (COEF_A * x_cur.astype(jnp.float32) + prod_mat).astype(jnp.bfloat16)
    return x_cur


def solution(mesh):
    dp_size = mesh.shape["dp"]
    tp_size = mesh.shape["tp"]

    def local_step(grad_local, mom_local, weight_local, learn_rate, decay_rate):
        grad_sum = lax.psum_scatter(grad_local[0], "dp", scatter_dimension=1, tiled=True)
        grad_mean = grad_sum / dp_size
        mom_new = MOMENTUM * mom_local + grad_mean
        update = (grad_mean + MOMENTUM * mom_new).astype(jnp.bfloat16)
        whole_rows = lax.all_to_all(update, "dp", split_axis=0, concat_axis=1, tiled=True)
        whole_mats = lax.all_gather(whole_rows, "tp", axis=2, tiled=True)
        row_count = whole_mats.shape[1]
        col_count = whole_mats.shape[2]
        ortho_mat = newton_schulz(whole_mats, row_count <= col_count)
        col_width = col_count // tp_size
        own_cols = lax.dynamic_slice_in_dim(ortho_mat, lax.axis_index("tp") * col_width, col_width, axis=2)
        ortho_rows = lax.all_to_all(own_cols, "dp", split_axis=1, concat_axis=0, tiled=True)
        out_scale = 0.2 * math.sqrt(max(row_count, col_count))
        rate_col = learn_rate[:, None, None]
        weight_new = weight_local - rate_col * (out_scale * ortho_rows.astype(jnp.float32) + decay_rate * weight_local)
        weight_full = lax.all_gather(weight_new.astype(jnp.bfloat16), "dp", axis=1, tiled=True)
        return mom_new, weight_new, weight_full

    return jax.shard_map(
        local_step,
        mesh=mesh,
        in_specs=(P(("rep", "dp"), None, None, "tp"), P("rep", "dp", "tp"), P("rep", "dp", "tp"), P("rep"), P()),
        out_specs=(P("rep", "dp", "tp"), P("rep", "dp", "tp"), P("rep", None, "tp")),
        check_vma=False,
    )
```

profile of v0, /device:TPU:1, one launch (start us, length us, event | category | flops | bytes accessed | tf_op | source)
XLA Modules:
  0.0 286.3 jit_solution(16811677034964053539)
XLA Ops:
  7.2 0.0 reduce-scatter.2.cloned.1.call-start
  7.2 0.7 reduce-scatter.2.cloned.1.call-update
  7.9 0.0 all-gather.3.cloned.1.call-start
  8.0 40.7 %reduce-scatter.2.cloned.1.call-done = f32[8,128,128]{2,1,0:T(8,128)} async-done(((f32[8,1024,128]{2,1,0:T(8,128)}), f32[8,128,128]{2,1,0:T(8,128)}) %reduce-scatter.2.cloned.1.call-update) | async-done | bytes 524304 | tf_op jit(solution)/shard_map/reduce_scatter | solution.py:40
  48.7 2.0 add_convert_fusion.5
  50.6 13.0 %all_to_all.21 = bf16[8,128,128]{2,1,0:T(8,128)(2,1)} all-to-all(bf16[8,128,128]{2,1,0:T(8,128)(2,1)S(1)} %get-tuple-element.5), channel_id=1, replica_groups=mesh['rep'=1,'tp'=16,'dp'=8] {'dp'}, dimensions={0} | all-to-all | bytes 524288 | tf_op jit(solution)/shard_map/all_to_all | solution.py:44
  63.6 0.0 all-gather.3.cloned.1.call-update
  63.7 55.0 %all-gather.3.cloned.1.call-done = bf16[1,1024,2048]{2,1,0:T(8,128)(2,1)} async-done(((bf16[1,1024,128]{2,1,0:T(8,128)(2,1)}), bf16[1,1024,2048]{2,1,0:T(8,128)(2,1)}) %all-gather.3.cloned.1.call-update) | async-done | bytes 4194320 | tf_op jit(solution)/shard_map/all_gather | solution.py:45
  118.6 4.9 %fusion = f32[]{:T(128)} fusion(bf16[1,1024,2048]{2,1,0:T(8,128)(2,1)} %all-gather.3.cloned.1.call-done), kind=kLoop, calls=%fused_computation.2 | loop fusion | flops 6291455 | bytes 4194308 | tf_op jit(solution)/shard_map/reduce_sum | solution.py:17
  124.3 8.0 %fusion.19 = bf16[1024,1024]{1,0:T(8,128)(2,1)S(1)} fusion(bf16[1,1024,2048]{2,1,0:T(8,128)(2,1)} %all-gather.3.cloned.1.call-done, f32[]{:T(128)S(6)} %add.55), kind=kOutput, calls=%fused_computation.26 | convolution fusion | flops 4301258752 | bytes 6291460 | tf_op jit(solution)/shard_map/bik,bjk->bij/dot_general | solution.py:21
  132.3 11.8 %fusion.5 = bf16[1,1024,2048]{2,1,0:T(8,128)(2,1)} fusion(f32[]{:T(128)S(6)} %add.55, bf16[1,1024,2048]{2,1,0:T(8,128)(2,1)} %all-gather.3.cloned.1.call-done, bf16[1024,1024]{1,0:T(8,128)(2,1)S(1)} %fusion.19), kind=kOutput, calls=%fused_computation.11 | convolution fusion | flops 6468665344 | bytes 10485764 | tf_op jit(solution)/shard_map/bij,bjk->bik/dot_general | solution.py:28
  144.1 8.0 %fusion.16 = bf16[1024,1024]{1,0:T(8,128)(2,1)S(1)} fusion(bf16[1,1024,2048]{2,1,0:T(8,128)(2,1)} %fusion.5), kind=kOutput, calls=%fused_computation.23 | convolution fusion | flops 4294967296 | bytes 6291456 | tf_op jit(solution)/shard_map/bik,bjk->bij/dot_general | solution.py:21
  152.1 11.9 %fusion.4 = bf16[1,1024,2048]{2,1,0:T(8,128)(2,1)} fusion(bf16[1,1024,2048]{2,1,0:T(8,128)(2,1)} %fusion.5, bf16[1024,1024]{1,0:T(8,128)(2,1)S(1)} %fusion.16), kind=kOutput, calls=%fused_computation.9 | convolution fusion | flops 6456082432 | bytes 10485760 | tf_op jit(solution)/shard_map/bij,bjk->bik/dot_general | solution.py:28
  164.0 8.0 %fusion.13 = bf16[1024,1024]{1,0:T(8,128)(2,1)S(1)} fusion(bf16[1,1024,2048]{2,1,0:T(8,128)(2,1)} %fusion.4), kind=kOutput, calls=%fused_computation.20 | convolution fusion | flops 4294967296 | bytes 6291456 | tf_op jit(solution)/shard_map/bik,bjk->bij/dot_general | solution.py:21
  172.0 11.6 %fusion.3 = bf16[1,1024,2048]{2,1,0:T(8,128)(2,1)} fusion(bf16[1,1024,2048]{2,1,0:T(8,128)(2,1)} %fusion.4, bf16[1024,1024]{1,0:T(8,128)(2,1)S(1)} %fusion.13), kind=kOutput, calls=%fused_computation.7 | convolution fusion | flops 6456082432 | bytes 10485760 | tf_op jit(solution)/shard_map/bij,bjk->bik/dot_general | solution.py:28
  183.6 8.0 %fusion.10 = bf16[1024,1024]{1,0:T(8,128)(2,1)S(1)} fusion(bf16[1,1024,2048]{2,1,0:T(8,128)(2,1)} %fusion.3), kind=kOutput, calls=%fused_computation.17 | convolution fusion | flops 4294967296 | bytes 6291456 | tf_op jit(solution)/shard_map/bik,bjk->bij/dot_general | solution.py:21
  191.6 21.5 %fusion.2 = bf16[1,1024,2048]{2,1,0:T(8,128)(2,1)} fusion(bf16[1,1024,2048]{2,1,0:T(8,128)(2,1)} %fusion.3, bf16[1024,1024]{1,0:T(8,128)(2,1)S(1)} %fusion.10), kind=kOutput, calls=%fused_computation.5 | convolution fusion | flops 6456082432 | bytes 10485760 | tf_op jit(solution)/shard_map/bij,bjk->bik/dot_general | solution.py:28
  213.1 8.0 %fusion.7 = bf16[1024,1024]{1,0:T(8,128)(2,1)S(1)} fusion(bf16[1,1024,2048]{2,1,0:T(8,128)(2,1)} %fusion.2), kind=kOutput, calls=%fused_computation.14 | convolution fusion | flops 4294967296 | bytes 6291456 | tf_op jit(solution)/shard_map/bik,bjk->bij/dot_general | solution.py:21
  221.1 12.2 %convolution_bitcast_fusion = f32[1,1024,2048]{2,1,0:T(8,128)} fusion(bf16[1,1024,2048]{2,1,0:T(8,128)(2,1)} %fusion.2, bf16[1024,1024]{1,0:T(8,128)(2,1)S(1)} %fusion.7), kind=kOutput, calls=%fused_computation.12 | convolution fusion | flops 6447693824 | bytes 14680064 | tf_op jit(solution)/shard_map/bij,bjk->bik/dot_general | solution.py:28
  233.3 1.2 fusion.28
  234.5 0.4 copy.10
  234.9 0.5 broadcast.71
  235.4 2.2 reduce.1
  237.7 0.8 reshape.129
  238.4 6.3 %all-to-all-start.1 = ((bf16[8,2,8192]{2,1,0:T(2,128)(2,1)}), bf16[8,2,8192]{2,1,0:T(2,128)(2,1)S(1)}, u32[]{:S(2)}, u32[]{:S(2)}) async-start(bf16[8,2,8192]{2,1,0:T(2,128)(2,1)} %reshape.129), calls=%async_computation.2 | async-start | bytes 524288 | tf_op jit(solution)/shard_map/all_to_all | solution.py:51
  245.4 5.6 %all-to-all-done.1 = bf16[8,2,8192]{2,1,0:T(2,128)(2,1)S(1)} async-done(((bf16[8,2,8192]{2,1,0:T(2,128)(2,1)}), bf16[8,2,8192]{2,1,0:T(2,128)(2,1)S(1)}, u32[]{:S(2)}, u32[]{:S(2)}) %all-to-all-start.1) | async-done | bytes 262176 | tf_op jit(solution)/shard_map/all_to_all | solution.py:51
  251.0 0.3 reshape.130
  251.3 0.7 convert_multiply_fusion.1
  252.1 1.0 fusion.33
  253.1 0.0 all-gather.5.cloned.1.call-update
  253.1 23.4 %all-gather.5.cloned.1.call-done = bf16[8,1024,128]{2,1,0:T(8,128)(2,1)} async-done(((bf16[8,128,128]{2,1,0:T(8,128)(2,1)}), bf16[8,1024,128]{2,1,0:T(8,128)(2,1)}) %all-gather.5.cloned.1.call-update) | async-done | bytes 2097168 | tf_op jit(solution)/shard_map/all_gather | solution.py:55
  276.6 3.1 %copy.13 = bf16[8,1024,128]{2,1,0:T(8,128)(2,1)} copy(bf16[8,1024,128]{2,1,0:T(8,128)(2,1)} %all-gather.5.cloned.1.call-done) | data formatting | bytes 4194304
  (7 shorter events, 0.0 us)
Async XLA Ops:
  7.2 41.5 %copy-start = (f32[8,128,128]{2,1,0:T(8,128)S(1)}, f32[8,128,128]{2,1,0:T(8,128)}, u32[]{:S(2)}) copy-start(f32[8,128,128]{2,1,0:T(8,128)} %param.6) | copy-start | bytes 1572868
  7.2 41.5 %reduce-scatter.2.cloned.1.call-start = ((), (), s32[]{:S(2)}) async-start(), calls=%async_computation.3 | async-start | bytes 4718592 | tf_op jit(solution)/shard_map/reduce_scatter | solution.py:40
  7.9 110.7 %all-gather.3.cloned.1.call-start = ((), (), s32[]{:S(2)}) async-start(), calls=%async_computation.4 | async-start | bytes 4456448 | tf_op jit(solution)/shard_map/all_gather | solution.py:45
  233.3 18.8 %copy-start.1 = (f32[8,128,128]{2,1,0:T(8,128)S(1)}, f32[8,128,128]{2,1,0:T(8,128)}, u32[]{:S(2)}) copy-start(f32[8,128,128]{2,1,0:T(8,128)} %param.7) | copy-start | bytes 1572868
  233.3 18.8 %copy-start.2 = (f32[8]{0:T(128)S(1)}, f32[8]{0:T(128)}, u32[]{:S(2)}) copy-start(f32[8]{0:T(128)} %param.8) | copy-start | bytes 100
  238.4 12.6 %all-to-all-start.1 = ((bf16[8,2,8192]{2,1,0:T(2,128)(2,1)}), bf16[8,2,8192]{2,1,0:T(2,128)(2,1)S(1)}, u32[]{:S(2)}, u32[]{:S(2)}) async-start(bf16[8,2,8192]{2,1,0:T(2,128)(2,1)} %reshape.129), calls=%async_computation.2 | async-start | bytes 524288 | tf_op jit(solution)/shard_map/all_to_all | solution.py:51
  244.8 31.8 %all-gather.5.cloned.1.call-start = ((), (), s32[]{:S(2)}) async-start(), calls=%async_computation.5 | async-start | bytes 2359296 | tf_op jit(solution)/shard_map/all_gather | solution.py:55
Sparse Core Ops, SparseCore 0:
  10.4 38.2 reduce-scatter.1
  63.8 54.8 all-gather.2
  253.2 23.2 all-gather.4
where the time goes:
time: 290 us; the launch traced here: 286 us
  waiting for transfers between devices  125 us (43%)
  matrix products  109 us (38%)
  between operations  15.4 us (5%)
  blocking collectives  13 us (4%)
  other arithmetic  12.1 us (4%)
  starting transfers between devices  6.4 us (2%)
  local copies, waits for them, and re-layouts  5.02 us (2%)
    dot_general x5, matrix products, newton_schulz(): jnp.einsum('bij,bjk->bik', poly_mat, x_cur, preferred_element_type=jnp.fl...  69 us
    all_gather x1, waiting for transfers between devices, local_step(): whole_mats = lax.all_gather(whole_rows, 'tp', axis=2, tiled=True)  55 us
    reduce_scatter x1, waiting for transfers between devices, local_step(): lax.psum_scatter(grad_local[0], 'dp', scatter_dimension=1, tiled=True)  40.7 us
    dot_general x5, matrix products, newton_schulz(): jnp.einsum('bik,bjk->bij', x_cur, x_cur, preferred_element_type=jnp.float32)  39.9 us
    all_gather x1, waiting for transfers between devices, local_step(): lax.all_gather(weight_new.astype(jnp.bfloat16), 'dp', axis=1, tiled=True)  23.4 us
    all_to_all x1, blocking collectives, local_step(): lax.all_to_all(update, 'dp', split_axis=0, concat_axis=1, tiled=True)  13 us
    all_to_all x1, starting transfers between devices, local_step(): lax.all_to_all(own_cols, 'dp', split_axis=1, concat_axis=0, tiled=True)  6.32 us
  transfers between devices with their start and end apart: 4, of which 4 were waited for; matrix products, arithmetic and copies ran while one was open for 0% of the time, Pallas kernels for 0%

commit v1 on v0

v1 whole, which is shorter than its diff:
```python
import math
import jax
import jax.numpy as jnp
from jax import lax
from jax.experimental import pallas as pl
from jax.experimental.pallas import tpu as pltpu
from jax.sharding import PartitionSpec as P

MOMENTUM = 0.95
NS_STEPS = 5
COEF_A = 3.4445
COEF_B = -4.7750
COEF_C = 2.0315
NORM_EPS = 1e-7
F32 = jnp.float32
BF16 = jnp.bfloat16

MATS, ROWS, COLS = 8, 1024, 2048
NC = 4
RC = 128 // NC
OUT_SCALE = 0.2 * math.sqrt(max(ROWS, COLS))


def dot_nt(lhs, rhs):
    return lax.dot_general(lhs, rhs, (((1,), (1,)), ((), ())), preferred_element_type=F32)


def dot_nn(lhs, rhs):
    return lax.dot_general(lhs, rhs, (((1,), (0,)), ((), ())), preferred_element_type=F32)


class Copies:
    def __init__(self, send_sems, recv_sems):
        self.send_sems, self.recv_sems = send_sems, recv_sems
        self.used = 0
        self.all = []

    def start(self, src, dst, **device):
        copy = pltpu.make_async_remote_copy(
            src_ref=src, dst_ref=dst, send_sem=self.send_sems.at[self.used], recv_sem=self.recv_sems.at[self.used],
            device_id=device, device_id_type=pl.DeviceIdType.MESH,
        )
        self.used += 1
        copy.start()
        self.all.append(copy)
        return copy


N_REMOTE = NC * (4 + 4 + 2 + 7 + 16) + 4 + 3 + 1 + 4 + 2 + 6
N_LOCAL = NC * 5 + 1 + 1 + 1 + 8 + 16


def muon_kernel(grad, mom, weight, rate, decay, mom_out, weight_out, full_out,
                own_g, sib_g, p2a, p1b, p1a, m2b, m1a, m1b, mom_v, upd, gath, sq_acc, x_cur, gram, poly,
                w_full, x_full, w_new, w_low, send_sems, recv_sems, local_sems):
    me = lax.axis_index("dp")
    tp = lax.axis_index("tp")
    x, core = lax.div(me, 2), lax.rem(me, 2)
    z, y = lax.div(tp, 4), lax.rem(tp, 4)
    xp, xm, x2 = lax.rem(x + 1, 4), lax.rem(x + 3, 4), lax.rem(x + 2, 4)
    yp, ym = lax.rem(y + 1, 4), lax.rem(y + 3, 4)
    zp, zm = lax.rem(z + 1, 4), lax.rem(z + 3, 4)
    sib = x * 2 + 1 - core
    dp_xp, dp_xm, dp_x2 = xp * 2 + core, xm * 2 + core, x2 * 2 + core
    tp_yp, tp_ym, tp_zp, tp_zm = z * 4 + yp, z * 4 + ym, zp * 4 + y, zm * 4 + y
    slots = (x2, xp, xm, x)

    rem = Copies(send_sems, recv_sems)
    n_local = [0]
    open_local = []

    def local(src, dst):
        copy = pltpu.make_async_copy(src, dst, local_sems.at[n_local[0]])
        n_local[0] += 1
        copy.start()
        return copy

    own_loads = {}
    for r in range(NC):
        for s in range(4):
            row = pl.multiple_of((slots[s] * 2 + core) * 128 + r * RC, RC)
            own_loads[r, s] = local(grad.at[0, :, pl.ds(row, RC), :], own_g.at[s, r])
    mom_load = local(mom, mom_v)

    barrier = pltpu.get_barrier_semaphore()
    for i in range(1, 8):
        pl.semaphore_signal(barrier, inc=1, device_id={"dp": lax.rem(me + i, 8)}, device_id_type=pl.DeviceIdType.MESH)
    for t in (tp_yp, tp_ym, tp_zp, tp_zm):
        pl.semaphore_signal(barrier, inc=1, device_id={"tp": t}, device_id_type=pl.DeviceIdType.MESH)
    pl.semaphore_wait(barrier, 11)

    d2d = {}
    for r in range(NC):
        for s in range(4):
            row = pl.multiple_of((slots[s] * 2 + 1 - core) * 128 + r * RC, RC)
            d2d[r, s] = rem.start(grad.at[0, :, pl.ds(row, RC), :], sib_g.at[s, r], dp=sib)

    st = {}

    def rs_raw(r):
        for s in (0, 1, 2):
            own_loads[r, s].wait()
            d2d[r, s].wait_recv()
            own_g[s, r] = own_g[s, r] + sib_g[s, r]
            if s == 0:
                st["p2a", r] = rem.start(own_g.at[0, r, pl.ds(0, 4)], p2a.at[r], dp=dp_xp)
                st["m2b", r] = rem.start(own_g.at[0, r, pl.ds(4, 4)], m2b.at[r], dp=dp_xm)
            if s == 1:
                st["p1b", r] = rem.start(own_g.at[1, r, pl.ds(4, 4)], p1b.at[r], dp=dp_xp)
            if s == 2:
                st["m1a", r] = rem.start(own_g.at[2, r, pl.ds(0, 4)], m1a.at[r], dp=dp_xm)

    def rs_sum(r):
        st["p2a", r].wait_recv()
        own_g[1, r, pl.ds(0, 4)] = own_g[1, r, pl.ds(0, 4)] + p2a[r]
        st["p1a", r] = rem.start(own_g.at[1, r, pl.ds(0, 4)], p1a.at[r], dp=dp_xp)
        st["m2b", r].wait_recv()
        own_g[2, r, pl.ds(4, 4)] = own_g[2, r, pl.ds(4, 4)] + m2b[r]
        st["m1b", r] = rem.start(own_g.at[2, r, pl.ds(4, 4)], m1b.at[r], dp=dp_xm)

    def update(r):
        own_loads[r, 3].wait()
        d2d[r, 3].wait_recv()
        if r == 0:
            mom_load.wait()
        for name in ("p1b", "m1a", "p1a", "m1b"):
            st[name, r].wait_recv()
        for half, (near, far) in enumerate(((m1a, p1a), (p1b, m1b))):
            js = pl.ds(half * 4, 4)
            total = (own_g[3, r, js] + sib_g[3, r, js]) + (near[r] + far[r])
            mean = total * (1.0 / 8.0)
            mom_new = MOMENTUM * mom_v[js, pl.ds(r * RC, RC)] + mean
            mom_v[js, pl.ds(r * RC, RC)] = mom_new
            upd[r, js] = (mean + MOMENTUM * mom_new).astype(BF16)
        st["own", r] = local(upd.at[r, me], gath.at[z, y, r, me])
        st["a2a", r] = [rem.start(upd.at[r, lax.rem(me + i, 8)], gath.at[z, y, r, me], dp=lax.rem(me + i, 8))
                        for i in range(1, 8)]

    lo, hi = pl.ds(0, 4), pl.ds(4, 4)

    def both(name, r, block, **axes):
        for key, device in axes.items():
            axis = "tp"
            st[name + key, r] = rem.start(block, block, **{axis: device})

    def gather1(r):
        st["own", r].wait()
        for copy in st["a2a", r]:
            copy.wait_recv()
        both("g1z", r, gath.at[z, y, r, lo], p=tp_zp, m=tp_zm)
        both("g1y", r, gath.at[z, y, r, hi], p=tp_yp, m=tp_ym)

    def forward1(r):
        st["g1zp", r].wait_recv()
        both("f1z", r, gath.at[zm, y, r, pl.ds(0, 2)], p=tp_zp)
        st["g1yp", r].wait_recv()
        both("f1y", r, gath.at[z, ym, r, pl.ds(4, 2)], p=tp_yp)
        st["g1zm", r].wait_recv()
        both("f1z", r, gath.at[zp, y, r, pl.ds(2, 2)], m=tp_zm)
        st["g1ym", r].wait_recv()
        both("f1y", r, gath.at[z, yp, r, pl.ds(6, 2)], m=tp_ym)

    def gather2(r):
        st["f1zp", r].wait_recv()
        st["f1zm", r].wait_recv()
        both("g2y", r, gath.at[:, y, r, lo], p=tp_yp, m=tp_ym)
        st["f1yp", r].wait_recv()
        st["f1ym", r].wait_recv()
        both("g2z", r, gath.at[z, :, r, hi], p=tp_zp, m=tp_zm)

    def forward2(r):
        st["g2yp", r].wait_recv()
        both("f2y", r, gath.at[:, ym, r, pl.ds(0, 2)], p=tp_yp)
        st["g2ym", r].wait_recv()
        both("f2y", r, gath.at[:, yp, r, pl.ds(2, 2)], m=tp_ym)
        st["g2zp", r].wait_recv()
        both("f2z", r, gath.at[zm, :, r, pl.ds(4, 2)], p=tp_zp)
        st["g2zm", r].wait_recv()
        both("f2z", r, gath.at[zp, :, r, pl.ds(6, 2)], m=tp_zm)

    def squares(r):
        for name in ("f2yp", "f2ym", "f2zp", "f2zm"):
            st[name, r].wait_recv()
        if r == 0:
            sq_acc[...] = jnp.zeros_like(sq_acc)

        @pl.loop(0, 4)
        def _(i):
            for j in range(4):
                block = gath[i, j, r].astype(F32)
                sq_acc[...] += jnp.sum((block * block).reshape(RC, 8, 128), axis=0)

    stages = (rs_raw, rs_sum, update, gather1, forward1, gather2, forward2, squares)
    for slot in range(NC + len(stages) - 1):
        for s, stage in enumerate(stages):
            if 0 <= slot - s < NC:
                stage(slot - s)

    mom_store = local(mom_v, mom_out)
    w_own = local(weight, w_full.at[:, me])
    w_send = [rem.start(weight, w_full.at[:, me], dp=d) for d in (dp_xp, dp_xm, dp_x2, sib)]
    base = rem.used
    w_fwd = []

    norm = jnp.sqrt(jnp.sum(sq_acc[...], keepdims=True))
    inv = 1.0 / (norm + NORM_EPS)

    @pl.loop(0, 4)
    def _(i):
        for j in range(4):
            cols = pl.ds(pl.multiple_of(i * 512 + j * 128, 128), 128)
            for r in range(NC):
                for d in range(8):
                    block = gath[i, j, r, d].astype(F32) * inv
                    x_cur[pl.ds(d * 128 + r * RC, RC), cols] = block.astype(BF16)

    def mirror_store(dst, block, first):
        dst[pl.ds(first, ROWS - first), pl.ds(first, 256)] = block
        if first + 256 < ROWS:
            dst[pl.ds(first, 256), pl.ds(first + 256, ROWS - first - 256)] = block[256:, :].T

    def polynomial():
        for first in range(0, ROWS, 256):
            below = pl.ds(first, ROWS - first)
            mirror_store(gram, dot_nt(x_cur[below, :], x_cur[pl.ds(first, 256), :]).astype(BF16), first)
        for first in range(0, ROWS, 256):
            below, cols = pl.ds(first, ROWS - first), pl.ds(first, 256)
            square = dot_nn(gram[below, :], gram[:, cols])
            mirror_store(poly, (COEF_B * gram[below, cols].astype(F32) + COEF_C * square).astype(BF16), first)

    @pl.loop(0, NS_STEPS - 1)
    def _(step):
        polynomial()
        for first in range(0, COLS, 256):
            cols = pl.ds(first, 256)
            block = x_cur[:, cols]
            prod = dot_nn(poly[...], block)
            x_cur[:, cols] = (COEF_A * block.astype(F32) + prod).astype(BF16)

    for i, d in enumerate((dp_xm, dp_xp, dp_x2)):
        w_send[i].wait_recv()
        w_fwd.append(rem.start(w_full.at[:, d], w_full.at[:, d], dp=sib))

    polynomial()
    own_cols = pl.ds(pl.multiple_of(tp * 128, 128), 128)
    block = x_cur[:, own_cols]
    x_full[me] = (COEF_A * block.astype(F32) + dot_nn(poly[...], block)).astype(BF16)

    top, bot = pl.ds(0, 512), pl.ds(512, 512)
    f_pt = rem.start(x_full.at[me, top], x_full.at[me, top], dp=dp_xp)
    f_mb = rem.start(x_full.at[me, bot], x_full.at[me, bot], dp=dp_xm)
    f_pb = rem.start(x_full.at[me, bot], x_full.at[me, bot], dp=dp_xp)
    f_mt = rem.start(x_full.at[me, top], x_full.at[me, top], dp=dp_xm)
    f_s = rem.start(x_full.at[me], x_full.at[me], dp=sib)

    w_own.wait()
    w_send[3].wait_recv()
    for copy in w_fwd:
        copy.wait_recv()
    stores = []

    def finish(mat):
        lr = rate[mat]
        dec = decay[0]
        wf = w_full[mat].reshape(ROWS, 128)
        new = wf - lr * (OUT_SCALE * x_full[mat].astype(F32) + dec * wf)
        w_low[mat] = new.astype(BF16)
        stores.append(local(w_low.at[mat], full_out.at[mat]))
        wo = w_full[mat, me]
        rows = pl.ds(pl.multiple_of(me * 128, 128), 128)
        w_new[mat] = wo - lr * (OUT_SCALE * x_full[mat, rows].astype(F32) + dec * wo)

    finish(me)
    f_pt.wait_recv()
    q_p = rem.start(x_full.at[dp_xm, top], x_full.at[dp_xm, top], dp=dp_xp)
    f_mb.wait_recv()
    q_m = rem.start(x_full.at[dp_xp, bot], x_full.at[dp_xp, bot], dp=dp_xm)
    f_s.wait_recv()
    finish(sib)
    f_pb.wait_recv()
    s_m = rem.start(x_full.at[dp_xm], x_full.at[dp_xm], dp=sib)
    f_mt.wait_recv()
    s_p = rem.start(x_full.at[dp_xp], x_full.at[dp_xp], dp=sib)
    finish(dp_xm)
    finish(dp_xp)
    s_m.wait_recv()
    finish(xm * 2 + 1 - core)
    s_p.wait_recv()
    finish(xp * 2 + 1 - core)
    q_p.wait_recv()
    s_t = rem.start(x_full.at[dp_x2, top], x_full.at[dp_x2, top], dp=sib)
    q_m.wait_recv()
    s_b = rem.start(x_full.at[dp_x2, bot], x_full.at[dp_x2, bot], dp=sib)
    finish(dp_x2)
    s_t.wait_recv()
    s_b.wait_recv()
    finish(x2 * 2 + 1 - core)
    stores.append(local(w_new, weight_out))
    for copy in rem.all:
        copy.wait_send()
    mom_store.wait()
    for copy in stores:
        copy.wait()


def solution(mesh):
    def local_step(grad_local, mom_local, weight_local, learn_rate, decay_rate):
        hbm = pl.BlockSpec(memory_space=pl.ANY)
        smem = pl.BlockSpec(memory_space=pltpu.SMEM)
        V = pltpu.VMEM
        return pl.pallas_call(
            muon_kernel,
            out_shape=(
                jax.ShapeDtypeStruct((8, 128, 128), F32),
                jax.ShapeDtypeStruct((8, 128, 128), F32),
                jax.ShapeDtypeStruct((8, 1024, 128), BF16),
            ),
            in_specs=[hbm, hbm, hbm, smem, smem],
            out_specs=(hbm, hbm, hbm),
            scratch_shapes=[
                V((4, NC, 8, RC, 128), F32), V((4, NC, 8, RC, 128), F32),
                V((NC, 4, RC, 128), F32), V((NC, 4, RC, 128), F32), V((NC, 4, RC, 128), F32),
                V((NC, 4, RC, 128), F32), V((NC, 4, RC, 128), F32), V((NC, 4, RC, 128), F32),
                V((8, 128, 128), F32), V((NC, 8, RC, 128), BF16),
                V((4, 4, NC, 8, RC, 128), BF16), V((8, 128), F32),
                V((ROWS, COLS), BF16), V((ROWS, ROWS), BF16), V((ROWS, ROWS), BF16),
                V((8, 8, 128, 128), F32), V((8, ROWS, 128), BF16), V((8, 128, 128), F32), V((8, ROWS, 128), BF16),
                pltpu.SemaphoreType.DMA((N_REMOTE,)), pltpu.SemaphoreType.DMA((N_REMOTE,)),
                pltpu.SemaphoreType.DMA((N_LOCAL,)),
            ],
            compiler_params=pltpu.CompilerParams(
                collective_id=0, has_side_effects=True, vmem_limit_bytes=58 * 2**20),
            name="muon_step",
        )(grad_local, mom_local, weight_local, learn_rate, decay_rate.reshape(1))

    return jax.shard_map(
        local_step,
        mesh=mesh,
        in_specs=(P(("rep", "dp"), None, None, "tp"), P("rep", "dp", "tp"), P("rep", "dp", "tp"), P("rep"), P()),
        out_specs=(P("rep", "dp", "tp"), P("rep", "dp", "tp"), P("rep", None, "tp")),
        check_vma=False,
    )
```

time: 290 us -> 119 us (0.41); the launches traced: 286 us -> 119 us
  waiting for transfers between devices: 125 us -> 0 us
  Pallas kernels: 0 us -> 112 us
  matrix products: 109 us -> 0 us
  between operations: 15.4 us -> 1.3 us
  blocking collectives: 13 us -> 0 us
  other arithmetic: 12.1 us -> 0 us
  starting transfers between devices: 6.4 us -> 0 us
    pallas_call x0 -> x1, Pallas kernels: none -> 112 us  [local_step(): pl.pallas_call(muon_kernel, out_shape=(jax.ShapeDtypeStruct((8, 128, 128)...]
    dot_general x10 -> x0, matrix products: 109 us -> none  [the longest x5 69 us: newton_schulz(): jnp.einsum('bij,bjk->bik', poly_mat, x_cur, preferred_element_type=jnp.fl...]
    all_gather x2 -> x0, waiting for transfers between devices: 78.4 us -> none  [the longest x1 55 us: local_step(): whole_mats = lax.all_gather(whole_rows, 'tp', axis=2, tiled=True)]
    reduce_scatter x1 -> x0, waiting for transfers between devices: 40.7 us -> none  [local_step(): lax.psum_scatter(grad_local[0], 'dp', scatter_dimension=1, tiled=True)]
    all_to_all x1 -> x0, blocking collectives: 13 us -> none  [local_step(): lax.all_to_all(update, 'dp', split_axis=0, concat_axis=1, tiled=True)]
    all_to_all x1 -> x0, starting transfers between devices: 6.32 us -> none  [local_step(): lax.all_to_all(own_cols, 'dp', split_axis=1, concat_axis=0, tiled=True)]
    all_to_all x1 -> x0, waiting for transfers between devices: 5.64 us -> none  [local_step(): lax.all_to_all(own_cols, 'dp', split_axis=1, concat_axis=0, tiled=True)]
    reduce_sum x1 -> x0, other arithmetic: 4.95 us -> none  [newton_schulz(): norm_val = jnp.sqrt(jnp.sum(upd_f32 * upd_f32, axis=(1, 2), keepdims=True))]
  transfers between devices with their start and end apart: 4 -> 0, of which waited for: 4 -> 0; matrix products, arithmetic and copies ran while one was open for 0% -> 0% of each run, Pallas kernels for 0% -> 0%
where the time goes in v1:
time: 119 us
  Pallas kernels  112 us (94%)
  local copies, waits for them, and re-layouts  5.21 us (4%)
  between operations  1.3 us (1%)
    pallas_call x1, Pallas kernels, local_step(): pl.pallas_call(muon_kernel, out_shape=(jax.ShapeDtypeStruct((8, 128, 128)...  112 us
    unnamed x5, local copies, waits for them, and re-layouts  5.21 us

profile of v1, /device:TPU:1, one launch (start us, length us, event | category | flops | bytes accessed | tf_op | source)
XLA Modules:
  0.0 118.5 jit_solution(14717997919099640190)
XLA Ops:
  1.3 112.0 %muon_step.1 = (f32[8,128,128]{2,1,0:T(8,128)}, f32[8,128,128]{2,1,0:T(8,128)}, bf16[8,1024,128]{2,1,0:T(8,128)(2,1)}) custom-call(f32[1,8,1024,128]{3,2,1,0:T(8,128)} %grad.1, f32[8,128,128]{2,1,0:T(8,128)} %mom.1, f32[8,128,128]{2,1,0:T(8,128)} %weight.1, f32[8]{0:T(128)} %rate.1, f32[1]{0:T(128)} %bitcast.1.decay), custom_call_target="tpu_custom_call" | custom-call | tf_op jit(solution)/shard_map/muon_step/pallas_call | solution.py:311
  113.3 0.0 copy-start
  113.3 2.0 %copy.12 = f32[8,128,128]{2,1,0:T(8,128)} copy(f32[8,128,128]{2,1,0:T(8,128)} %get-tuple-element.6) | data formatting | bytes 1048576
  115.3 1.9 %copy.13 = f32[8,128,128]{2,1,0:T(8,128)} copy(f32[8,128,128]{2,1,0:T(8,128)} %get-tuple-element.7) | data formatting | bytes 1048576
  117.2 0.0 copy-done
  117.2 1.3 %copy.14 = bf16[8,1024,128]{2,1,0:T(8,128)(2,1)} copy(bf16[8,1024,128]{2,1,0:T(8,128)(2,1)S(1)} %copy-done) | data formatting | bytes 4194304
Async XLA Ops:
  113.3 3.9 %copy-start = (bf16[8,1024,128]{2,1,0:T(8,128)(2,1)S(1)}, bf16[8,1024,128]{2,1,0:T(8,128)(2,1)}, u32[]{:S(2)}) copy-start(bf16[8,1024,128]{2,1,0:T(8,128)(2,1)} %get-tuple-element.8) | copy-start | bytes 6291460

commit v2 on v0

v2 whole, which is shorter than its diff:
```python
import math
import jax
import jax.numpy as jnp
from jax import lax
from jax.experimental import pallas as pl
from jax.experimental.pallas import tpu as pltpu
from jax.sharding import PartitionSpec as P

MOMENTUM = 0.95
NS_STEPS = 5
COEF_A = 3.4445
COEF_B = -4.7750
COEF_C = 2.0315
NORM_EPS = 1e-7
F32 = jnp.float32
BF16 = jnp.bfloat16

MATS, ROWS, COLS = 8, 1024, 2048
NC = 8
RC = 128 // NC
OUT_SCALE = 0.2 * math.sqrt(max(ROWS, COLS))


def dot_nt(lhs, rhs):
    return lax.dot_general(lhs, rhs, (((1,), (1,)), ((), ())), preferred_element_type=F32)


def dot_nn(lhs, rhs):
    return lax.dot_general(lhs, rhs, (((1,), (0,)), ((), ())), preferred_element_type=F32)


ORDER = (
    ("dd", 0), ("dd", 1), ("dd", 2), ("dd", 3), ("far", 0), ("far", 1), ("near", 1), ("near", 0), ("dd", 4),
    ("far", 2), ("sum", 0), ("far", 3), ("sum", 1), ("near", 2), ("dd", 6), ("sum", 2), ("update", 0), ("far", 4),
    ("near", 3), ("sum", 3), ("update", 1), ("update", 2), ("dd", 5), ("near", 4), ("dd", 7), ("sum", 4), ("far", 5),
    ("gather1", 0), ("update", 3), ("near", 5), ("far", 6), ("gather1", 1), ("gather1", 2), ("near", 6), ("far", 7),
    ("sum", 5), ("gather2", 0), ("gather1", 3), ("update", 4), ("sum", 6), ("gather2", 1), ("near", 7), ("sum", 7),
    ("update", 5), ("gather2", 2), ("gather1", 4), ("forward2", 0), ("update", 6), ("gather2", 3), ("update", 7),
    ("gather1", 5), ("forward2", 2), ("gather1", 6), ("forward2", 1), ("gather1", 7), ("gather2", 4), ("gather2", 5),
    ("gather2", 6), ("gather2", 7), ("squares", 0), ("forward2", 5), ("forward2", 3), ("forward2", 4),
    ("forward2", 6), ("forward2", 7), ("squares", 1), ("squares", 5), ("squares", 4), ("squares", 2), ("squares", 6),
    ("squares", 3), ("squares", 7),
)

CHUNK_GROUPS = ("dd0", "dd1", "p2", "p1", "a2a", "g1", "g2", "f2")
LATE_GROUPS = ("w3", "w4", "fa", "fb", "fs", "s1", "q", "s2")
SEND_GROUPS = ("dd", "rs", "a2a", "g1", "g2", "f2", "w3", "w4", "last")
N_RECV = NC * len(CHUNK_GROUPS) + len(LATE_GROUPS)
N_LOCAL = NC + 2


def muon_kernel(grad, mom, weight, rate, decay, mom_out, weight_out, full_out,
                own_g, sib_g, p2a, p1b, p1a, m2b, m1a, m1b, upd, gath, sq_acc, x_cur, gram, poly,
                w_full, x_full, send_sems, recv_sems, local_sems):
    me = lax.axis_index("dp")
    tp = lax.axis_index("tp")
    x, core = lax.div(me, 2), lax.rem(me, 2)
    z, y = lax.div(tp, 4), lax.rem(tp, 4)
    xp, xm, x2 = lax.rem(x + 1, 4), lax.rem(x + 3, 4), lax.rem(x + 2, 4)
    yp, ym, y2 = lax.rem(y + 1, 4), lax.rem(y + 3, 4), lax.rem(y + 2, 4)
    zp, zm, z2 = lax.rem(z + 1, 4), lax.rem(z + 3, 4), lax.rem(z + 2, 4)
    sib = x * 2 + 1 - core
    dp_xp, dp_xm, dp_x2 = xp * 2 + core, xm * 2 + core, x2 * 2 + core
    tp_yp, tp_ym, tp_y2 = z * 4 + yp, z * 4 + ym, z * 4 + y2
    tp_zp, tp_zm, tp_z2 = zp * 4 + y, zm * 4 + y, z2 * 4 + y
    slots = (x2, xp, xm, x)

    def recv_sem(group, r=None):
        if r is None:
            return recv_sems.at[NC * len(CHUNK_GROUPS) + LATE_GROUPS.index(group)]
        return recv_sems.at[r * len(CHUNK_GROUPS) + CHUNK_GROUPS.index(group)]

    def send(src, dst, sent, group, r=None, **device):
        pltpu.make_async_remote_copy(
            src_ref=src, dst_ref=dst, send_sem=send_sems.at[SEND_GROUPS.index(sent)], recv_sem=recv_sem(group, r),
            device_id=device, device_id_type=pl.DeviceIdType.MESH,
        ).start()

    def drain(sem, like):
        pltpu.make_async_copy(like, like, sem).wait()

    def arrived(like, group, r=None):
        drain(recv_sem(group, r), like)

    for r in range(NC):
        for s in range(4):
            row = pl.multiple_of((slots[s] * 2 + core) * 128 + r * RC, RC)
            pltpu.make_async_copy(grad.at[0, :, pl.ds(row, RC), :], own_g.at[s, r], local_sems.at[r]).start()
    mom_load = pltpu.make_async_copy(mom, mom_out, local_sems.at[NC])
    mom_load.start()

    barrier = pltpu.get_barrier_semaphore()
    for i in range(1, 8):
        pl.semaphore_signal(barrier, inc=1, device_id={"dp": lax.rem(me + i, 8)}, device_id_type=pl.DeviceIdType.MESH)
    for t in (tp_yp, tp_ym, tp_y2, tp_zp, tp_zm, tp_z2):
        pl.semaphore_signal(barrier, inc=1, device_id={"tp": t}, device_id_type=pl.DeviceIdType.MESH)
    with jax.named_scope("entry"):
        pl.semaphore_wait(barrier, 13)

    def dd(r):
        for s in range(4):
            row = pl.multiple_of((slots[s] * 2 + 1 - core) * 128 + r * RC, RC)
            send(grad.at[0, :, pl.ds(row, RC), :], sib_g.at[s, r], "dd", "dd1" if s else "dd0", r, dp=sib)

    lo, hi = pl.ds(0, 4), pl.ds(4, 4)

    def far(r):
        drain(local_sems.at[r], own_g.at[:, r])
        arrived(sib_g.at[0, r], "dd0", r)
        own_g[0, r] = own_g[0, r] + sib_g[0, r]
        send(own_g.at[0, r, lo], p2a.at[r], "rs", "p2", r, dp=dp_xp)
        send(own_g.at[0, r, hi], m2b.at[r], "rs", "p2", r, dp=dp_xm)

    def near(r):
        arrived(sib_g.at[pl.ds(1, 3), r], "dd1", r)
        own_g[1, r] = own_g[1, r] + sib_g[1, r]
        send(own_g.at[1, r, hi], p1b.at[r], "rs", "p1", r, dp=dp_xp)
        own_g[2, r] = own_g[2, r] + sib_g[2, r]
        send(own_g.at[2, r, lo], m1a.at[r], "rs", "p1", r, dp=dp_xm)

    def sum_(r):
        arrived(own_g.at[0, r], "p2", r)
        own_g[1, r, lo] = own_g[1, r, lo] + p2a[r]
        send(own_g.at[1, r, lo], p1a.at[r], "rs", "p1", r, dp=dp_xp)
        own_g[2, r, hi] = own_g[2, r, hi] + m2b[r]
        send(own_g.at[2, r, hi], m1b.at[r], "rs", "p1", r, dp=dp_xm)

    waited = []

    def update(r):
        if not waited:
            mom_load.wait()
            waited.append(r)
        arrived(own_g.at[pl.ds(0, 2), r], "p1", r)
        for half, (near_ref, far_ref) in enumerate(((m1a, p1a), (p1b, m1b))):
            js = pl.ds(half * 4, 4)
            total = (own_g[3, r, js] + sib_g[3, r, js]) + (near_ref[r] + far_ref[r])
            mean = total * (1.0 / 8.0)
            mom_new = MOMENTUM * mom_out[js, pl.ds(r * RC, RC)] + mean
            mom_out[js, pl.ds(r * RC, RC)] = mom_new
            upd[r, js] = (mean + MOMENTUM * mom_new).astype(BF16)
        for i in range(1, 8):
            to = lax.rem(me + i, 8)
            send(upd.at[r, to], gath.at[z, y, r, me], "a2a", "a2a", r, dp=to)
        gath[z, y, r, me] = upd[r, me]

    def gather1(r):
        arrived(upd.at[r, pl.ds(0, 7)], "a2a", r)
        for near_first in ((tp_zp, tp_yp), (tp_zm, tp_ym), (tp_z2, tp_y2)):
            send(gath.at[z, y, r, lo], gath.at[z, y, r, lo], "g1", "g1", r, tp=near_first[0])
            send(gath.at[z, y, r, hi], gath.at[z, y, r, hi], "g1", "g1", r, tp=near_first[1])

    def gather2(r):
        arrived(gath.at[0, pl.ds(0, 3), r], "g1", r)
        for t in (tp_yp, tp_ym):
            send(gath.at[:, y, r, lo], gath.at[:, y, r, lo], "g2", "g2", r, tp=t)
        for t in (tp_zp, tp_zm):
            send(gath.at[z, :, r, hi], gath.at[z, :, r, hi], "g2", "g2", r, tp=t)

    def forward2(r):
        arrived(gath.at[pl.ds(0, 2), :, r], "g2", r)
        for block, t in ((gath.at[:, ym, r, pl.ds(0, 2)], tp_yp), (gath.at[:, yp, r, pl.ds(2, 2)], tp_ym),
                         (gath.at[zm, :, r, pl.ds(4, 2)], tp_zp), (gath.at[zp, :, r, pl.ds(6, 2)], tp_zm)):
            send(block, block, "f2", "f2", r, tp=t)

    def squares(r):
        arrived(gath.at[0, :, r], "f2", r)

        @pl.loop(0, 4)
        def _(i):
            for j in range(4):
                block = gath[i, j, r].astype(F32)
                sq_acc[...] += jnp.sum((block * block).reshape(RC, 8, 128), axis=0)

    sq_acc[...] = jnp.zeros_like(sq_acc)
    stages = {"dd": dd, "far": far, "near": near, "sum": sum_, "update": update, "gather1": gather1,
              "gather2": gather2, "forward2": forward2, "squares": squares}
    for name, r in ORDER:
        with jax.named_scope(f"{name}_{r}"):
            stages[name](r)

    w_own = pltpu.make_async_copy(weight, w_full.at[:, me], local_sems.at[NC + 1])
    w_own.start()
    for d in (dp_xp, dp_xm, dp_x2):
        send(weight, w_full.at[:, me], "w3", "w3", dp=d)
    send(weight, w_full.at[:, me], "w4", "w4", dp=sib)

    norm = jnp.sqrt(jnp.sum(sq_acc[...], keepdims=True))
    inv = 1.0 / (norm + NORM_EPS)

    @pl.loop(0, 4)
    def _(i):
        for j in range(4):
            cols = pl.ds(pl.multiple_of(i * 512 + j * 128, 128), 128)
            for r in range(NC):
                for d in range(8):
                    block = gath[i, j, r, d].astype(F32) * inv
                    x_cur[pl.ds(d * 128 + r * RC, RC), cols] = block.astype(BF16)

    def mirror_store(dst, block, first):
        dst[pl.ds(first, ROWS - first), pl.ds(first, 256)] = block
        if first + 256 < ROWS:
            dst[pl.ds(first, 256), pl.ds(first + 256, ROWS - first - 256)] = block[256:, :].T

    def polynomial():
        for first in range(0, ROWS, 256):
            below = pl.ds(first, ROWS - first)
            mirror_store(gram, dot_nt(x_cur[below, :], x_cur[pl.ds(first, 256), :]).astype(BF16), first)
        for first in range(0, ROWS, 256):
            below, cols = pl.ds(first, ROWS - first), pl.ds(first, 256)
            square = dot_nn(gram[below, :], gram[:, cols])
            mirror_store(poly, (COEF_B * gram[below, cols].astype(F32) + COEF_C * square).astype(BF16), first)

    @pl.loop(0, NS_STEPS - 1)
    def _(step):
        polynomial()
        for first in range(0, COLS, 256):
            cols = pl.ds(first, 256)
            block = x_cur[:, cols]
            prod = dot_nn(poly[...], block)
            x_cur[:, cols] = (COEF_A * block.astype(F32) + prod).astype(BF16)

    arrived(w_full.at[:, pl.ds(0, 3)], "w3")
    for d in (dp_xm, dp_xp, dp_x2):
        send(w_full.at[:, d], w_full.at[:, d], "w4", "w4", dp=sib)

    polynomial()
    own_cols = pl.ds(pl.multiple_of(tp * 128, 128), 128)
    top, bot = pl.ds(0, 512), pl.ds(512, 512)
    block = x_cur[:, own_cols]

    def last(group, src, **device):
        send(src, src, "last", group, **device)

    for rows, first, second in ((top, dp_xp, "fa"), (bot, dp_xm, "fa")):
        x_full[me, rows] = (COEF_A * x_cur[rows, own_cols].astype(F32) + dot_nn(poly[rows, :], block)).astype(BF16)
        last(second, x_full.at[me, rows], dp=first)
    last("fb", x_full.at[me, bot], dp=dp_xp)
    last("fb", x_full.at[me, top], dp=dp_xm)
    last("fs", x_full.at[me], dp=sib)

    w_own.wait()
    arrived(w_full.at[:, pl.ds(0, 4)], "w4")

    def finish(mat):
        lr = rate[mat]
        dec = decay[0]
        wf = w_full[mat].reshape(ROWS, 128)
        new = wf - lr * (OUT_SCALE * x_full[mat].astype(F32) + dec * wf)
        full_out[mat] = new.astype(BF16)
        wo = w_full[mat, me]
        rows = pl.ds(pl.multiple_of(me * 128, 128), 128)
        weight_out[mat] = wo - lr * (OUT_SCALE * x_full[mat, rows].astype(F32) + dec * wo)

    pair = x_full.at[0]
    finish(me)
    arrived(pair, "fa")
    last("q", x_full.at[dp_xm, top], dp=dp_xp)
    last("q", x_full.at[dp_xp, bot], dp=dp_xm)
    arrived(pair, "fs")
    finish(sib)
    arrived(pair, "fb")
    last("s1", x_full.at[dp_xm], dp=sib)
    last("s1", x_full.at[dp_xp], dp=sib)
    finish(dp_xm)
    finish(dp_xp)
    arrived(x_full.at[pl.ds(0, 2)], "s1")
    finish(xm * 2 + 1 - core)
    finish(xp * 2 + 1 - core)
    arrived(pair, "q")
    last("s2", x_full.at[dp_x2, top], dp=sib)
    last("s2", x_full.at[dp_x2, bot], dp=sib)
    finish(dp_x2)
    arrived(pair, "s2")
    finish(x2 * 2 + 1 - core)

    with jax.named_scope("sends"):
        for group, like in (("dd", own_g), ("rs", own_g.at[pl.ds(0, 3)]), ("a2a", upd.at[:, pl.ds(0, 7)]),
                            ("g1", gath.at[0, pl.ds(0, 3)]), ("g2", gath.at[pl.ds(0, 2)]), ("f2", gath.at[0]),
                            ("w3", w_full.at[:, pl.ds(0, 3)]), ("w4", w_full.at[:, pl.ds(0, 4)]),
                            ("last", x_full.at[pl.ds(0, 7)])):
            drain(send_sems.at[SEND_GROUPS.index(group)], like)


def solution(mesh):
    def local_step(grad_local, mom_local, weight_local, learn_rate, decay_rate):
        hbm = pl.BlockSpec(memory_space=pltpu.HBM)
        vmem = pl.BlockSpec(memory_space=pltpu.VMEM)
        smem = pl.BlockSpec(memory_space=pltpu.SMEM)
        V = pltpu.VMEM
        return pl.pallas_call(
            muon_kernel,
            out_shape=(
                V((8, 128, 128), F32),
                V((8, 128, 128), F32),
                V((8, 1024, 128), BF16),
            ),
            in_specs=[hbm, hbm, hbm, smem, smem],
            out_specs=(vmem, vmem, vmem),
            scratch_shapes=[
                V((4, NC, 8, RC, 128), F32), V((4, NC, 8, RC, 128), F32),
                V((NC, 4, RC, 128), F32), V((NC, 4, RC, 128), F32), V((NC, 4, RC, 128), F32),
                V((NC, 4, RC, 128), F32), V((NC, 4, RC, 128), F32), V((NC, 4, RC, 128), F32),
                V((NC, 8, RC, 128), BF16),
                V((4, 4, NC, 8, RC, 128), BF16), V((8, 128), F32),
                V((ROWS, COLS), BF16), V((ROWS, ROWS), BF16), V((ROWS, ROWS), BF16),
                V((8, 8, 128, 128), F32), V((8, ROWS, 128), BF16),
                pltpu.SemaphoreType.DMA((len(SEND_GROUPS),)), pltpu.SemaphoreType.DMA((N_RECV,)),
                pltpu.SemaphoreType.DMA((N_LOCAL,)),
            ],
            compiler_params=pltpu.CompilerParams(
                collective_id=0, has_side_effects=True, vmem_limit_bytes=63_400_000),
            name="muon_step",
        )(grad_local, mom_local, weight_local, learn_rate, decay_rate.reshape(1))

    return jax.shard_map(
        local_step,
        mesh=mesh,
        in_specs=(P(("rep", "dp"), None, None, "tp"), P("rep", "dp", "tp"), P("rep", "dp", "tp"), P("rep"), P()),
        out_specs=(P("rep", "dp", "tp"), P("rep", "dp", "tp"), P("rep", None, "tp")),
        check_vma=False,
    )
```

time: 290 us -> 108 us (0.37); the launches traced: 286 us -> 107 us
  waiting for transfers between devices: 125 us -> 0 us
  matrix products: 109 us -> 0 us
  Pallas kernels: 0 us -> 103 us
  between operations: 15.4 us -> 1.29 us
  blocking collectives: 13 us -> 0 us
  other arithmetic: 12.1 us -> 0 us
  starting transfers between devices: 6.4 us -> 0 us
    dot_general x10 -> x0, matrix products: 109 us -> none  [the longest x5 69 us: newton_schulz(): jnp.einsum('bij,bjk->bik', poly_mat, x_cur, preferred_element_type=jnp.fl...]
    pallas_call x0 -> x1, Pallas kernels: none -> 103 us  [local_step(): pl.pallas_call(muon_kernel, out_shape=(V((8, 128, 128), F32), V((8, 128,...]
    all_gather x2 -> x0, waiting for transfers between devices: 78.4 us -> none  [the longest x1 55 us: local_step(): whole_mats = lax.all_gather(whole_rows, 'tp', axis=2, tiled=True)]
    reduce_scatter x1 -> x0, waiting for transfers between devices: 40.7 us -> none  [local_step(): lax.psum_scatter(grad_local[0], 'dp', scatter_dimension=1, tiled=True)]
    all_to_all x1 -> x0, blocking collectives: 13 us -> none  [local_step(): lax.all_to_all(update, 'dp', split_axis=0, concat_axis=1, tiled=True)]
    all_to_all x1 -> x0, starting transfers between devices: 6.32 us -> none  [local_step(): lax.all_to_all(own_cols, 'dp', split_axis=1, concat_axis=0, tiled=True)]
    all_to_all x1 -> x0, waiting for transfers between devices: 5.64 us -> none  [local_step(): lax.all_to_all(own_cols, 'dp', split_axis=1, concat_axis=0, tiled=True)]
    reduce_sum x1 -> x0, other arithmetic: 4.95 us -> none  [newton_schulz(): norm_val = jnp.sqrt(jnp.sum(upd_f32 * upd_f32, axis=(1, 2), keepdims=True))]
  transfers between devices with their start and end apart: 4 -> 0, of which waited for: 4 -> 0; matrix products, arithmetic and copies ran while one was open for 0% -> 0% of each run, Pallas kernels for 0% -> 0%
where the time goes in v2:
time: 108 us; the launch traced here: 107 us
  Pallas kernels  103 us (95%)
  local copies, waits for them, and re-layouts  2.91 us (3%)
  between operations  1.29 us (1%)
    pallas_call x1, Pallas kernels, local_step(): pl.pallas_call(muon_kernel, out_shape=(V((8, 128, 128), F32), V((8, 128,...  103 us
    unnamed x3, local copies, waits for them, and re-layouts  2.91 us

profile of v2, /device:TPU:1, one launch (start us, length us, event | category | flops | bytes accessed | tf_op | source)
XLA Modules:
  0.0 107.4 jit_solution(567858732262930768)
XLA Ops:
  1.3 103.2 %muon_step.1 = (f32[8,128,128]{2,1,0:T(8,128)S(1)}, f32[8,128,128]{2,1,0:T(8,128)S(1)}, bf16[8,1024,128]{2,1,0:T(8,128)(2,1)S(1)}) custom-call(f32[1,8,1024,128]{3,2,1,0:T(8,128)} %grad.1, f32[8,128,128]{2,1,0:T(8,128)} %mom.1, f32[8,128,128]{2,1,0:T(8,128)} %weight.1, f32[8]{0:T(128)} %rate.1, f32[1]{0:T(128)} %bitcast.1.decay), custom_call_target="tpu_custom_call" | custom-call | tf_op jit(solution)/shard_map/muon_step/pallas_call | solution.py:291
  104.5 0.8 copy.11
  105.3 0.8 copy.12
  106.1 1.3 %copy.13 = bf16[8,1024,128]{2,1,0:T(8,128)(2,1)} copy(bf16[8,1024,128]{2,1,0:T(8,128)(2,1)S(1)} %get-tuple-element.5) | data formatting | bytes 4194304

commit v3 on v2

v3 whole, which is shorter than its diff:
```python
import math
import jax
import jax.numpy as jnp
from jax import lax
from jax.experimental import pallas as pl
from jax.experimental.pallas import tpu as pltpu
from jax.sharding import PartitionSpec as P

MOMENTUM = 0.95
NS_STEPS = 5
COEF_A = 3.4445
COEF_B = -4.7750
COEF_C = 2.0315
NORM_EPS = 1e-7
F32 = jnp.float32
BF16 = jnp.bfloat16

MATS, ROWS, COLS = 8, 1024, 2048
NC = 8
RC = 128 // NC
CR = 8 * RC
OUT_SCALE = 0.2 * math.sqrt(max(ROWS, COLS))


def dot_nt(lhs, rhs):
    return lax.dot_general(lhs, rhs, (((1,), (1,)), ((), ())), preferred_element_type=F32)


def dot_nn(lhs, rhs):
    return lax.dot_general(lhs, rhs, (((1,), (0,)), ((), ())), preferred_element_type=F32)


ORDER = (
    ("mom", 0), ("dd", 4), ("mom", 1), ("dd", 0), ("dd", 2), ("mom", 2), ("dd", 1), ("far", 0), ("dd", 5),
    ("near", 0), ("far", 2), ("far", 1), ("dd", 7), ("near", 2), ("near", 1), ("sum", 0), ("dd", 3), ("far", 4),
    ("sum", 2), ("sum", 1), ("far", 5), ("near", 5), ("far", 3), ("far", 7), ("gather1", 0), ("near", 3),
    ("gather1", 2), ("mom", 3), ("dd", 6), ("far", 6), ("mom", 4), ("gather1", 1), ("sum", 3), ("gather2", 0),
    ("near", 4), ("mom", 5), ("sum", 4), ("sum", 5), ("gather2", 2), ("near", 6), ("gather2", 1), ("gather1", 3),
    ("mom", 6), ("forward2", 0), ("mom", 7), ("sum", 6), ("near", 7), ("forward2", 2), ("sum", 7), ("gather1", 4),
    ("gather1", 5), ("forward2", 1), ("gather2", 3), ("gather1", 6), ("gather1", 7), ("gather2", 4), ("gather2", 5),
    ("gather2", 6), ("gather2", 7), ("forward2", 3), ("norm", 0), ("forward2", 5), ("scale", 2), ("scale", 1),
    ("forward2", 4), ("forward2", 6), ("scale", 0), ("gram", 0), ("forward2", 7), ("scale", 3), ("gram", 1),
    ("scale", 5), ("scale", 4), ("gram", 2), ("scale", 6), ("scale", 7), ("gram", 3),
)

CHUNK_GROUPS = ("dd0", "dd1", "p2", "p1", "mom", "g1", "g2", "f2")
LATE_GROUPS = ("sq", "back", "w3", "w4", "fa", "fb", "fs", "s1", "q", "s2")
SEND_GROUPS = ("dd", "rs", "mom", "back", "sq", "g1", "g2", "f2", "w3", "w4", "last")
N_RECV = NC * len(CHUNK_GROUPS) + len(LATE_GROUPS)
N_LOCAL = NC + 2


def muon_kernel(grad, mom, weight, rate, decay, mom_out, weight_out, full_out,
                own_g, sib_g, p2a, p1b, p1a, m2b, m1a, m1b, mom_x, mom_y, mom_r, gath, sq_own, sq_all,
                x_cur, gram, poly, w_full, x_full, send_sems, recv_sems, local_sems):
    me = lax.axis_index("dp")
    tp = lax.axis_index("tp")
    x, core = lax.div(me, 2), lax.rem(me, 2)
    z, y = lax.div(tp, 4), lax.rem(tp, 4)
    xp, xm, x2 = lax.rem(x + 1, 4), lax.rem(x + 3, 4), lax.rem(x + 2, 4)
    yp, ym, y2 = lax.rem(y + 1, 4), lax.rem(y + 3, 4), lax.rem(y + 2, 4)
    zp, zm, z2 = lax.rem(z + 1, 4), lax.rem(z + 3, 4), lax.rem(z + 2, 4)
    sib = x * 2 + 1 - core
    dp_xp, dp_xm, dp_x2 = xp * 2 + core, xm * 2 + core, x2 * 2 + core
    tp_yp, tp_ym, tp_y2 = z * 4 + yp, z * 4 + ym, z * 4 + y2
    tp_zp, tp_zm, tp_z2 = zp * 4 + y, zm * 4 + y, z2 * 4 + y
    slots = (x2, xp, xm, x)

    def recv_sem(group, r=None):
        if r is None:
            return recv_sems.at[NC * len(CHUNK_GROUPS) + LATE_GROUPS.index(group)]
        return recv_sems.at[r * len(CHUNK_GROUPS) + CHUNK_GROUPS.index(group)]

    def send(src, dst, sent, group, r=None, **device):
        pltpu.make_async_remote_copy(
            src_ref=src, dst_ref=dst, send_sem=send_sems.at[SEND_GROUPS.index(sent)], recv_sem=recv_sem(group, r),
            device_id=device, device_id_type=pl.DeviceIdType.MESH,
        ).start()

    def drain(sem, like):
        pltpu.make_async_copy(like, like, sem).wait()

    def arrived(like, group, r=None):
        drain(recv_sem(group, r), like)

    def peers(rest=7):
        return [lax.rem(me + i, 8) for i in range(1, rest + 1)]

    tp_peers = [lax.rem(tp + i, 16) for i in range(1, 16)]

    for r in range(NC):
        for s in range(4):
            pltpu.make_async_copy(grad.at[slots[s] * 2 + core, :, pl.ds(r * RC, RC), :], own_g.at[s, r],
                                  local_sems.at[r]).start()
        pltpu.make_async_copy(mom.at[me, pl.ds(r * RC, RC), :], mom_x.at[r, me], local_sems.at[NC]).start()

    barrier = pltpu.get_barrier_semaphore()
    for d in peers():
        pl.semaphore_signal(barrier, inc=1, device_id={"dp": d}, device_id_type=pl.DeviceIdType.MESH)
    for t in tp_peers:
        pl.semaphore_signal(barrier, inc=1, device_id={"tp": t}, device_id_type=pl.DeviceIdType.MESH)
    with jax.named_scope("entry"):
        pl.semaphore_wait(barrier, 22)

    def mom_(r):
        for d in peers():
            send(mom.at[d, pl.ds(r * RC, RC), :], mom_x.at[r, me], "mom", "mom", r, dp=d)

    def dd(r):
        for s in range(4):
            send(grad.at[slots[s] * 2 + 1 - core, :, pl.ds(r * RC, RC), :], sib_g.at[s, r], "dd", "dd1" if s else "dd0",
                 r, dp=sib)

    lo, hi = pl.ds(0, 4), pl.ds(4, 4)

    def far(r):
        drain(local_sems.at[r], own_g.at[:, r])
        arrived(sib_g.at[0, r], "dd0", r)
        own_g[0, r] = own_g[0, r] + sib_g[0, r]
        send(own_g.at[0, r, lo], p2a.at[r], "rs", "p2", r, dp=dp_xp)
        send(own_g.at[0, r, hi], m2b.at[r], "rs", "p2", r, dp=dp_xm)

    def near(r):
        arrived(sib_g.at[pl.ds(1, 3), r], "dd1", r)
        own_g[1, r] = own_g[1, r] + sib_g[1, r]
        send(own_g.at[1, r, hi], p1b.at[r], "rs", "p1", r, dp=dp_xp)
        own_g[2, r] = own_g[2, r] + sib_g[2, r]
        send(own_g.at[2, r, lo], m1a.at[r], "rs", "p1", r, dp=dp_xm)

    def sum_(r):
        arrived(own_g.at[0, r], "p2", r)
        own_g[1, r, lo] = own_g[1, r, lo] + p2a[r]
        send(own_g.at[1, r, lo], p1a.at[r], "rs", "p1", r, dp=dp_xp)
        own_g[2, r, hi] = own_g[2, r, hi] + m2b[r]
        send(own_g.at[2, r, hi], m1b.at[r], "rs", "p1", r, dp=dp_xm)

    started = []

    def gather1(r):
        if not started:
            drain(local_sems.at[NC], mom_x.at[:, 0])
            sq_own[...] = jnp.zeros_like(sq_own)
        started.append(r)
        arrived(own_g.at[pl.ds(0, 2), r], "p1", r)
        arrived(mom_x.at[r, pl.ds(0, 7)], "mom", r)
        for half, (near_ref, far_ref) in enumerate(((m1a, p1a), (p1b, m1b))):
            ds = pl.ds(half * 4, 4)
            total = (own_g[3, r, ds] + sib_g[3, r, ds]) + (near_ref[r] + far_ref[r])
            mean = total * (1.0 / 8.0)
            mom_new = MOMENTUM * mom_x[r, ds] + mean
            mom_y[ds, pl.ds(r * RC, RC)] = mom_new
            upd = (mean + MOMENTUM * mom_new).astype(BF16)
            gath[z, y, r, ds] = upd
            upd = upd.astype(F32)
            sq_own[...] += jnp.sum((upd * upd).reshape(RC // 2, 8, 128), axis=0)
        for near_first in ((tp_zp, tp_yp), (tp_zm, tp_ym), (tp_z2, tp_y2)):
            send(gath.at[z, y, r, lo], gath.at[z, y, r, lo], "g1", "g1", r, tp=near_first[0])
            send(gath.at[z, y, r, hi], gath.at[z, y, r, hi], "g1", "g1", r, tp=near_first[1])
        if len(started) == NC:
            for t in tp_peers:
                send(sq_own, sq_all.at[tp], "sq", "sq", tp=t)

    def gather2(r):
        arrived(gath.at[0, pl.ds(0, 3), r], "g1", r)
        for t in (tp_yp, tp_ym):
            send(gath.at[:, y, r, lo], gath.at[:, y, r, lo], "g2", "g2", r, tp=t)
        for t in (tp_zp, tp_zm):
            send(gath.at[z, :, r, hi], gath.at[z, :, r, hi], "g2", "g2", r, tp=t)

    def forward2(r):
        arrived(gath.at[pl.ds(0, 2), :, r], "g2", r)
        for block, t in ((gath.at[:, ym, r, pl.ds(0, 2)], tp_yp), (gath.at[:, yp, r, pl.ds(2, 2)], tp_ym),
                         (gath.at[zm, :, r, pl.ds(4, 2)], tp_zp), (gath.at[zp, :, r, pl.ds(6, 2)], tp_zm)):
            send(block, block, "f2", "f2", r, tp=t)

    inv = []

    def norm(_):
        sq_all[tp] = sq_own[...]
        arrived(sq_all.at[pl.ds(0, 15)], "sq")
        total = jnp.sum(jnp.sum(sq_all[...], axis=0), keepdims=True)
        inv.append(1.0 / (jnp.sqrt(total) + NORM_EPS))

    def scale(r):
        arrived(gath.at[0, :, r], "f2", r)
        for i in range(4):
            for j in range(4):
                block = gath[i, j, r].reshape(CR, 128).astype(F32) * inv[0]
                x_cur[pl.ds(r * CR, CR), pl.ds(i * 512 + j * 128, 128)] = block.astype(BF16)

    def mirror_store(dst, block, first):
        dst[pl.ds(0, first + 256), pl.ds(first, 256)] = block
        if first:
            dst[pl.ds(first, 256), pl.ds(0, first)] = block[:first, :].T

    def gram_(i):
        first = i * 256
        mirror_store(gram, dot_nt(x_cur[pl.ds(0, first + 256), :], x_cur[pl.ds(first, 256), :]).astype(BF16), first)

    stages = {"mom": mom_, "dd": dd, "far": far, "near": near, "sum": sum_, "gather1": gather1, "gather2": gather2,
              "forward2": forward2, "norm": norm, "scale": scale, "gram": gram_}
    for name, r in ORDER:
        with jax.named_scope(f"{name}_{r}"):
            stages[name](r)

    w_own = pltpu.make_async_copy(weight, w_full.at[:, me], local_sems.at[NC + 1])
    w_own.start()
    for d in (dp_xp, dp_xm, dp_x2):
        send(weight, w_full.at[:, me], "w3", "w3", dp=d)
    send(weight, w_full.at[:, me], "w4", "w4", dp=sib)

    for d in peers():
        send(mom_y.at[d], mom_r.at[me], "back", "back", dp=d)

    def polynomial():
        for first in range(0, ROWS, 256):
            above, cols = pl.ds(0, first + 256), pl.ds(first, 256)
            square = dot_nn(gram[above, :], gram[:, cols])
            mirror_store(poly, (COEF_B * gram[above, cols].astype(F32) + COEF_C * square).astype(BF16), first)

    @pl.loop(0, NS_STEPS - 1)
    def _(step):
        polynomial()
        for first in range(0, COLS, 256):
            cols = pl.ds(first, 256)
            block = x_cur[:, cols]
            prod = dot_nn(poly[...], block)
            x_cur[:, cols] = (COEF_A * block.astype(F32) + prod).astype(BF16)
        for i in range(4):
            gram_(i)

    arrived(w_full.at[:, pl.ds(0, 3)], "w3")
    for d in (dp_xm, dp_xp, dp_x2):
        send(w_full.at[:, d], w_full.at[:, d], "w4", "w4", dp=sib)

    polynomial()
    own_cols = pl.ds(pl.multiple_of(tp * 128, 128), 128)
    block = x_cur[:, own_cols]

    def last(group, src, **device):
        send(src, src, "last", group, **device)

    final = (COEF_A * block.astype(F32) + dot_nn(poly[...], block)).astype(BF16)
    for r in range(NC):
        for d in range(8):
            x_full[me, pl.ds(d * 128 + r * RC, RC)] = final[r * CR + d * RC:r * CR + (d + 1) * RC]
    top, bot = pl.ds(0, 512), pl.ds(512, 512)
    last("fa", x_full.at[me, top], dp=dp_xp)
    last("fa", x_full.at[me, bot], dp=dp_xm)
    last("fb", x_full.at[me, bot], dp=dp_xp)
    last("fb", x_full.at[me, top], dp=dp_xm)
    last("fs", x_full.at[me], dp=sib)

    w_own.wait()
    arrived(w_full.at[:, pl.ds(0, 4)], "w4")

    def finish(mat):
        lr = rate[mat]
        dec = decay[0]
        wf = w_full[mat].reshape(ROWS, 128)
        new = wf - lr * (OUT_SCALE * x_full[mat].astype(F32) + dec * wf)
        full_out[mat] = new.astype(BF16)
        wo = w_full[mat, me]
        rows = pl.ds(pl.multiple_of(me * 128, 128), 128)
        weight_out[mat] = wo - lr * (OUT_SCALE * x_full[mat, rows].astype(F32) + dec * wo)

    mom_r[me] = mom_y[me]
    arrived(mom_r.at[pl.ds(0, 7)], "back")
    mom_out[...] = mom_r[...]

    pair = x_full.at[0]
    finish(me)
    arrived(pair, "fa")
    last("q", x_full.at[dp_xm, top], dp=dp_xp)
    last("q", x_full.at[dp_xp, bot], dp=dp_xm)
    arrived(pair, "fs")
    finish(sib)
    arrived(pair, "fb")
    last("s1", x_full.at[dp_xm], dp=sib)
    last("s1", x_full.at[dp_xp], dp=sib)
    finish(dp_xm)
    finish(dp_xp)
    arrived(x_full.at[pl.ds(0, 2)], "s1")
    finish(xm * 2 + 1 - core)
    finish(xp * 2 + 1 - core)
    arrived(pair, "q")
    last("s2", x_full.at[dp_x2, top], dp=sib)
    last("s2", x_full.at[dp_x2, bot], dp=sib)
    finish(dp_x2)
    arrived(pair, "s2")
    finish(x2 * 2 + 1 - core)

    with jax.named_scope("sends"):
        for group, like in (("dd", own_g), ("rs", own_g.at[pl.ds(0, 3)]), ("mom", mom_x.at[:, pl.ds(0, 7)]),
                            ("back", mom_r.at[pl.ds(0, 7)]), ("sq", sq_all.at[pl.ds(0, 15)]), ("g1", gath.at[0, pl.ds(0, 3)]), ("g2", gath.at[pl.ds(0, 2)]), ("f2", gath.at[0]),
                            ("w3", w_full.at[:, pl.ds(0, 3)]), ("w4", w_full.at[:, pl.ds(0, 4)]),
                            ("last", x_full.at[pl.ds(0, 7)])):
            drain(send_sems.at[SEND_GROUPS.index(group)], like)


def solution(mesh):
    def local_step(grad_local, mom_local, weight_local, learn_rate, decay_rate):
        hbm = pl.BlockSpec(memory_space=pltpu.HBM)
        vmem = pl.BlockSpec(memory_space=pltpu.VMEM)
        smem = pl.BlockSpec(memory_space=pltpu.SMEM)
        V = pltpu.VMEM
        return pl.pallas_call(
            muon_kernel,
            out_shape=(
                V((8, 128, 128), F32),
                V((8, 128, 128), F32),
                V((8, 1024, 128), BF16),
            ),
            in_specs=[hbm, hbm, hbm, smem, smem],
            out_specs=(vmem, vmem, vmem),
            scratch_shapes=[
                V((4, NC, 8, RC, 128), F32), V((4, NC, 8, RC, 128), F32),
                V((NC, 4, RC, 128), F32), V((NC, 4, RC, 128), F32), V((NC, 4, RC, 128), F32),
                V((NC, 4, RC, 128), F32), V((NC, 4, RC, 128), F32), V((NC, 4, RC, 128), F32),
                V((NC, 8, RC, 128), F32), V((8, 128, 128), F32), V((8, 128, 128), F32),
                V((4, 4, NC, 8, RC, 128), BF16), V((8, 128), F32), V((16, 8, 128), F32),
                V((ROWS, COLS), BF16), V((ROWS, ROWS), BF16), V((ROWS, ROWS), BF16),
                V((8, 8, 128, 128), F32), V((8, ROWS, 128), BF16),
                pltpu.SemaphoreType.DMA((len(SEND_GROUPS),)), pltpu.SemaphoreType.DMA((N_RECV,)),
                pltpu.SemaphoreType.DMA((N_LOCAL,)),
            ],
            compiler_params=pltpu.CompilerParams(
                collective_id=0, has_side_effects=True, vmem_limit_bytes=63_400_000),
            name="muon_step",
        )(grad_local.reshape(8, 8, 128, 128), mom_local, weight_local, learn_rate, decay_rate.reshape(1))

    return jax.shard_map(
        local_step,
        mesh=mesh,
        in_specs=(P(("rep", "dp"), None, None, "tp"), P("rep", "dp", "tp"), P("rep", "dp", "tp"), P("rep"), P()),
        out_specs=(P("rep", "dp", "tp"), P("rep", "dp", "tp"), P("rep", None, "tp")),
        check_vma=False,
    )
```

time: 108 us -> 111 us (1.028)
  Pallas kernels: 103 us -> 106 us
    pallas_call x1, Pallas kernels: 103 us -> 106 us  [local_step(): pl.pallas_call(muon_kernel, out_shape=(V((8, 128, 128), F32), V((8, 128,...]
where the time goes in v3:
time: 111 us
  Pallas kernels  106 us (95%)
  local copies, waits for them, and re-layouts  2.91 us (3%)
  between operations  1.29 us (1%)
    pallas_call x1, Pallas kernels, local_step(): pl.pallas_call(muon_kernel, out_shape=(V((8, 128, 128), F32), V((8, 128,...  106 us
    unnamed x3, local copies, waits for them, and re-layouts  2.91 us

profile of v3, /device:TPU:1, one launch (start us, length us, event | category | flops | bytes accessed | tf_op | source)
XLA Modules:
  0.0 110.5 jit_solution(277517827354132633)
XLA Ops:
  1.3 106.3 %muon_step.1 = (f32[8,128,128]{2,1,0:T(8,128)S(1)}, f32[8,128,128]{2,1,0:T(8,128)S(1)}, bf16[8,1024,128]{2,1,0:T(8,128)(2,1)S(1)}) custom-call(f32[8,8,128,128]{3,2,1,0:T(8,128)} %bitcast.3, f32[8,128,128]{2,1,0:T(8,128)} %mom.1, f32[8,128,128]{2,1,0:T(8,128)} %weight.1, f32[8]{0:T(128)} %rate.1, f32[1]{0:T(128)} %bitcast.2.decay), custom_call_target="tpu_custom_call" | custom-call | tf_op jit(solution)/shard_map/muon_step/pallas_call | solution.py:307
  107.6 0.8 copy.11
  108.4 0.8 copy.12
  109.2 1.3 %copy.13 = bf16[8,1024,128]{2,1,0:T(8,128)(2,1)} copy(bf16[8,1024,128]{2,1,0:T(8,128)(2,1)S(1)} %get-tuple-element.5) | data formatting | bytes 4194304

commit v4 on v3

--- a/solution.py
+++ b/solution.py
@@ -31,27 +31,27 @@
 
 
 ORDER = (
-    ("mom", 0), ("dd", 4), ("mom", 1), ("dd", 0), ("dd", 2), ("mom", 2), ("dd", 1), ("far", 0), ("dd", 5),
-    ("near", 0), ("far", 2), ("far", 1), ("dd", 7), ("near", 2), ("near", 1), ("sum", 0), ("dd", 3), ("far", 4),
-    ("sum", 2), ("sum", 1), ("far", 5), ("near", 5), ("far", 3), ("far", 7), ("gather1", 0), ("near", 3),
-    ("gather1", 2), ("mom", 3), ("dd", 6), ("far", 6), ("mom", 4), ("gather1", 1), ("sum", 3), ("gather2", 0),
-    ("near", 4), ("mom", 5), ("sum", 4), ("sum", 5), ("gather2", 2), ("near", 6), ("gather2", 1), ("gather1", 3),
-    ("mom", 6), ("forward2", 0), ("mom", 7), ("sum", 6), ("near", 7), ("forward2", 2), ("sum", 7), ("gather1", 4),
-    ("gather1", 5), ("forward2", 1), ("gather2", 3), ("gather1", 6), ("gather1", 7), ("gather2", 4), ("gather2", 5),
-    ("gather2", 6), ("gather2", 7), ("forward2", 3), ("norm", 0), ("forward2", 5), ("scale", 2), ("scale", 1),
-    ("forward2", 4), ("forward2", 6), ("scale", 0), ("gram", 0), ("forward2", 7), ("scale", 3), ("gram", 1),
-    ("scale", 5), ("scale", 4), ("gram", 2), ("scale", 6), ("scale", 7), ("gram", 3),
+    ("mom", 1), ("dd", 0), ("dd", 1), ("far", 0), ("far", 1), ("dd", 4), ("mom", 0), ("mom", 4), ("dd", 7),
+    ("near", 0), ("dd", 5), ("dd", 3), ("near", 1), ("far", 3), ("dd", 6), ("sum", 1), ("sum", 0), ("mom", 2),
+    ("dd", 2), ("far", 5), ("mom", 3), ("far", 6), ("gather1", 1), ("far", 2), ("far", 4), ("gather1", 0),
+    ("near", 3), ("sum", 3), ("mom", 6), ("near", 2), ("gather2", 1), ("sum", 2), ("near", 4), ("mom", 7), ("sum", 4),
+    ("gather2", 0), ("gather1", 3), ("far", 7), ("near", 7), ("near", 6), ("near", 5), ("mom", 5), ("gather1", 2),
+    ("forward2", 1), ("sum", 6), ("gather1", 4), ("sum", 7), ("forward2", 0), ("gather2", 3), ("sum", 5),
+    ("gather2", 2), ("gather1", 6), ("gather1", 7), ("gather1", 5), ("forward2", 3), ("gather2", 4), ("gather2", 6),
+    ("gather2", 5), ("sums", 0), ("gather2", 7), ("forward2", 2), ("forward2", 4), ("forward2", 5), ("forward2", 6),
+    ("norm", 0), ("forward2", 7), ("scale", 0), ("scale", 3), ("scale", 1), ("scale", 2), ("gram", 0), ("gram", 1),
+    ("scale", 4), ("scale", 5), ("gram", 2), ("scale", 6), ("scale", 7), ("gram", 3),
 )
 
 CHUNK_GROUPS = ("dd0", "dd1", "p2", "p1", "mom", "g1", "g2", "f2")
-LATE_GROUPS = ("sq", "back", "w3", "w4", "fa", "fb", "fs", "s1", "q", "s2")
-SEND_GROUPS = ("dd", "rs", "mom", "back", "sq", "g1", "g2", "f2", "w3", "w4", "last")
+LATE_GROUPS = ("sqz", "sqy", "back", "w3", "w4", "fa", "fb", "fs", "s1", "q", "s2")
+SEND_GROUPS = ("dd", "rs", "mom", "back", "sq", "g1", "g2", "w3", "w4", "last")
 N_RECV = NC * len(CHUNK_GROUPS) + len(LATE_GROUPS)
 N_LOCAL = NC + 2
 
 
 def muon_kernel(grad, mom, weight, rate, decay, mom_out, weight_out, full_out,
-                own_g, sib_g, p2a, p1b, p1a, m2b, m1a, m1b, mom_x, mom_y, mom_r, gath, sq_own, sq_all,
+                own_g, sib_g, p2a, p1b, p1a, m2b, m1a, m1b, mom_x, mom_y, mom_r, gath, sq_own, sq_z, sq_y,
                 x_cur, gram, poly, w_full, x_full, send_sems, recv_sems, local_sems):
     me = lax.axis_index("dp")
     tp = lax.axis_index("tp")
@@ -86,21 +86,19 @@
     def peers(rest=7):
         return [lax.rem(me + i, 8) for i in range(1, rest + 1)]
 
-    tp_peers = [lax.rem(tp + i, 16) for i in range(1, 16)]
-
+    barrier = pltpu.get_barrier_semaphore()
+    for d in peers():
+        pl.semaphore_signal(barrier, inc=1, device_id={"dp": d}, device_id_type=pl.DeviceIdType.MESH)
+    for t in (tp_yp, tp_ym, tp_y2, tp_zp, tp_zm, tp_z2):
+        pl.semaphore_signal(barrier, inc=1, device_id={"tp": t}, device_id_type=pl.DeviceIdType.MESH)
     for r in range(NC):
         for s in range(4):
             pltpu.make_async_copy(grad.at[slots[s] * 2 + core, :, pl.ds(r * RC, RC), :], own_g.at[s, r],
                                   local_sems.at[r]).start()
         pltpu.make_async_copy(mom.at[me, pl.ds(r * RC, RC), :], mom_x.at[r, me], local_sems.at[NC]).start()
 
-    barrier = pltpu.get_barrier_semaphore()
-    for d in peers():
-        pl.semaphore_signal(barrier, inc=1, device_id={"dp": d}, device_id_type=pl.DeviceIdType.MESH)
-    for t in tp_peers:
-        pl.semaphore_signal(barrier, inc=1, device_id={"tp": t}, device_id_type=pl.DeviceIdType.MESH)
     with jax.named_scope("entry"):
-        pl.semaphore_wait(barrier, 22)
+        pl.semaphore_wait(barrier, 13)
 
     def mom_(r):
         for d in peers():
@@ -157,8 +155,8 @@
             send(gath.at[z, y, r, lo], gath.at[z, y, r, lo], "g1", "g1", r, tp=near_first[0])
             send(gath.at[z, y, r, hi], gath.at[z, y, r, hi], "g1", "g1", r, tp=near_first[1])
         if len(started) == NC:
-            for t in tp_peers:
-                send(sq_own, sq_all.at[tp], "sq", "sq", tp=t)
+            for t in (tp_zp, tp_zm, tp_z2):
+                send(sq_own, sq_z.at[z], "sq", "sqz", tp=t)
 
     def gather2(r):
         arrived(gath.at[0, pl.ds(0, 3), r], "g1", r)
@@ -171,14 +169,20 @@
         arrived(gath.at[pl.ds(0, 2), :, r], "g2", r)
         for block, t in ((gath.at[:, ym, r, pl.ds(0, 2)], tp_yp), (gath.at[:, yp, r, pl.ds(2, 2)], tp_ym),
                          (gath.at[zm, :, r, pl.ds(4, 2)], tp_zp), (gath.at[zp, :, r, pl.ds(6, 2)], tp_zm)):
-            send(block, block, "f2", "f2", r, tp=t)
+            send(block, block, "g2", "f2", r, tp=t)
 
     inv = []
 
+    def sums(_):
+        sq_z[z] = sq_own[...]
+        arrived(sq_z.at[pl.ds(0, 3)], "sqz")
+        sq_y[y] = jnp.sum(sq_z[...], axis=0)
+        for t in (tp_yp, tp_ym, tp_y2):
+            send(sq_y.at[y], sq_y.at[y], "sq", "sqy", tp=t)
+
     def norm(_):
-        sq_all[tp] = sq_own[...]
-        arrived(sq_all.at[pl.ds(0, 15)], "sq")
-        total = jnp.sum(jnp.sum(sq_all[...], axis=0), keepdims=True)
+        arrived(sq_y.at[pl.ds(0, 3)], "sqy")
+        total = jnp.sum(jnp.sum(sq_y[...], axis=0), keepdims=True)
         inv.append(1.0 / (jnp.sqrt(total) + NORM_EPS))
 
     def scale(r):
@@ -188,17 +192,20 @@
                 block = gath[i, j, r].reshape(CR, 128).astype(F32) * inv[0]
                 x_cur[pl.ds(r * CR, CR), pl.ds(i * 512 + j * 128, 128)] = block.astype(BF16)
 
+    def gram_rows(i):
+        rows, left = pl.ds(i * 256, 256), pl.ds(0, i * 256)
+        block = dot_nt(x_cur[rows, :], x_cur[pl.ds(0, i * 256 + 256), :]).astype(BF16)
+        gram[rows, pl.ds(0, i * 256 + 256)] = block
+        if i:
+            gram[left, rows] = block[:, :i * 256].T
+
     def mirror_store(dst, block, first):
-        dst[pl.ds(0, first + 256), pl.ds(first, 256)] = block
-        if first:
-            dst[pl.ds(first, 256), pl.ds(0, first)] = block[:first, :].T
-
-    def gram_(i):
-        first = i * 256
-        mirror_store(gram, dot_nt(x_cur[pl.ds(0, first + 256), :], x_cur[pl.ds(first, 256), :]).astype(BF16), first)
+        dst[pl.ds(first, ROWS - first), pl.ds(first, 256)] = block
+        if first + 256 < ROWS:
+            dst[pl.ds(first, 256), pl.ds(first + 256, ROWS - first - 256)] = block[256:, :].T
 
     stages = {"mom": mom_, "dd": dd, "far": far, "near": near, "sum": sum_, "gather1": gather1, "gather2": gather2,
-              "forward2": forward2, "norm": norm, "scale": scale, "gram": gram_}
+              "forward2": forward2, "norm": norm, "scale": scale, "sums": sums, "gram": gram_rows}
     for name, r in ORDER:
         with jax.named_scope(f"{name}_{r}"):
             stages[name](r)
@@ -214,9 +221,9 @@
 
     def polynomial():
         for first in range(0, ROWS, 256):
-            above, cols = pl.ds(0, first + 256), pl.ds(first, 256)
-            square = dot_nn(gram[above, :], gram[:, cols])
-            mirror_store(poly, (COEF_B * gram[above, cols].astype(F32) + COEF_C * square).astype(BF16), first)
+            below, cols = pl.ds(first, ROWS - first), pl.ds(first, 256)
+            square = dot_nn(gram[below, :], gram[:, cols])
+            mirror_store(poly, (COEF_B * gram[below, cols].astype(F32) + COEF_C * square).astype(BF16), first)
 
     @pl.loop(0, NS_STEPS - 1)
     def _(step):
@@ -226,8 +233,9 @@
             block = x_cur[:, cols]
             prod = dot_nn(poly[...], block)
             x_cur[:, cols] = (COEF_A * block.astype(F32) + prod).astype(BF16)
-        for i in range(4):
-            gram_(i)
+        for first in range(0, ROWS, 256):
+            below = pl.ds(first, ROWS - first)
+            mirror_store(gram, dot_nt(x_cur[below, :], x_cur[pl.ds(first, 256), :]).astype(BF16), first)
 
     arrived(w_full.at[:, pl.ds(0, 3)], "w3")
     for d in (dp_xm, dp_xp, dp_x2):
@@ -254,6 +262,10 @@
     w_own.wait()
     arrived(w_full.at[:, pl.ds(0, 4)], "w4")
 
+    def sent(*pairs):
+        for group, like in pairs:
+            drain(send_sems.at[SEND_GROUPS.index(group)], like)
+
     def finish(mat):
         lr = rate[mat]
         dec = decay[0]
@@ -270,6 +282,9 @@
 
     pair = x_full.at[0]
     finish(me)
+    sent(("dd", own_g), ("rs", own_g.at[pl.ds(0, 3)]), ("mom", mom_x.at[:, pl.ds(0, 7)]),
+         ("back", mom_r.at[pl.ds(0, 7)]), ("sq", mom_r.at[0, pl.ds(0, 48)]), ("g1", gath.at[0, pl.ds(0, 3)]),
+         ("g2", gath.at[pl.ds(0, 3)]), ("w3", w_full.at[:, pl.ds(0, 3)]), ("w4", w_full.at[:, pl.ds(0, 4)]))
     arrived(pair, "fa")
     last("q", x_full.at[dp_xm, top], dp=dp_xp)
     last("q", x_full.at[dp_xp, bot], dp=dp_xm)
@@ -290,12 +305,7 @@
     arrived(pair, "s2")
     finish(x2 * 2 + 1 - core)
 
-    with jax.named_scope("sends"):
-        for group, like in (("dd", own_g), ("rs", own_g.at[pl.ds(0, 3)]), ("mom", mom_x.at[:, pl.ds(0, 7)]),
-                            ("back", mom_r.at[pl.ds(0, 7)]), ("sq", sq_all.at[pl.ds(0, 15)]), ("g1", gath.at[0, pl.ds(0, 3)]), ("g2", gath.at[pl.ds(0, 2)]), ("f2", gath.at[0]),
-                            ("w3", w_full.at[:, pl.ds(0, 3)]), ("w4", w_full.at[:, pl.ds(0, 4)]),
-                            ("last", x_full.at[pl.ds(0, 7)])):
-            drain(send_sems.at[SEND_GROUPS.index(group)], like)
+    sent(("last", x_full.at[pl.ds(0, 7)]))
 
 
 def solution(mesh):
@@ -318,7 +328,7 @@
                 V((NC, 4, RC, 128), F32), V((NC, 4, RC, 128), F32), V((NC, 4, RC, 128), F32),
                 V((NC, 4, RC, 128), F32), V((NC, 4, RC, 128), F32), V((NC, 4, RC, 128), F32),
                 V((NC, 8, RC, 128), F32), V((8, 128, 128), F32), V((8, 128, 128), F32),
-                V((4, 4, NC, 8, RC, 128), BF16), V((8, 128), F32), V((16, 8, 128), F32),
+                V((4, 4, NC, 8, RC, 128), BF16), V((8, 128), F32), V((4, 8, 128), F32), V((4, 8, 128), F32),
                 V((ROWS, COLS), BF16), V((ROWS, ROWS), BF16), V((ROWS, ROWS), BF16),
                 V((8, 8, 128, 128), F32), V((8, ROWS, 128), BF16),
                 pltpu.SemaphoreType.DMA((len(SEND_GROUPS),)), pltpu.SemaphoreType.DMA((N_RECV,)),

time: 111 us -> 104 us (0.937)
  Pallas kernels: 106 us -> 99.2 us
    pallas_call x1, Pallas kernels: 106 us -> 99.2 us  [local_step(): pl.pallas_call(muon_kernel, out_shape=(V((8, 128, 128), F32), V((8, 128,...]
where the time goes in v4:
time: 104 us; the launch traced here: 103 us
  Pallas kernels  99.2 us (95%)
  local copies, waits for them, and re-layouts  2.91 us (3%)
  between operations  1.29 us (1%)
    pallas_call x1, Pallas kernels, local_step(): pl.pallas_call(muon_kernel, out_shape=(V((8, 128, 128), F32), V((8, 128,...  99.2 us
    unnamed x3, local copies, waits for them, and re-layouts  2.91 us

profile of v4, /device:TPU:1, one launch (start us, length us, event | category | flops | bytes accessed | tf_op | source)
XLA Modules:
  0.0 103.4 jit_solution(18348660816683876063)
XLA Ops:
  1.3 99.2 %muon_step.1 = (f32[8,128,128]{2,1,0:T(8,128)S(1)}, f32[8,128,128]{2,1,0:T(8,128)S(1)}, bf16[8,1024,128]{2,1,0:T(8,128)(2,1)S(1)}) custom-call(f32[8,8,128,128]{3,2,1,0:T(8,128)} %bitcast.3, f32[8,128,128]{2,1,0:T(8,128)} %mom.1, f32[8,128,128]{2,1,0:T(8,128)} %weight.1, f32[8]{0:T(128)} %rate.1, f32[1]{0:T(128)} %bitcast.2.decay), custom_call_target="tpu_custom_call" | custom-call | tf_op jit(solution)/shard_map/muon_step/pallas_call | solution.py:317
  100.5 0.8 copy.11
  101.3 0.8 copy.12
  102.1 1.3 %copy.13 = bf16[8,1024,128]{2,1,0:T(8,128)(2,1)} copy(bf16[8,1024,128]{2,1,0:T(8,128)(2,1)S(1)} %get-tuple-element.5) | data formatting | bytes 4194304

commit v5 on v4

--- a/solution.py
+++ b/solution.py
@@ -19,6 +19,7 @@
 NC = 8
 RC = 128 // NC
 CR = 8 * RC
+MIX = MOMENTUM * MOMENTUM / (1.0 + MOMENTUM)
 OUT_SCALE = 0.2 * math.sqrt(max(ROWS, COLS))
 
 
@@ -31,27 +32,26 @@
 
 
 ORDER = (
-    ("mom", 1), ("dd", 0), ("dd", 1), ("far", 0), ("far", 1), ("dd", 4), ("mom", 0), ("mom", 4), ("dd", 7),
-    ("near", 0), ("dd", 5), ("dd", 3), ("near", 1), ("far", 3), ("dd", 6), ("sum", 1), ("sum", 0), ("mom", 2),
-    ("dd", 2), ("far", 5), ("mom", 3), ("far", 6), ("gather1", 1), ("far", 2), ("far", 4), ("gather1", 0),
-    ("near", 3), ("sum", 3), ("mom", 6), ("near", 2), ("gather2", 1), ("sum", 2), ("near", 4), ("mom", 7), ("sum", 4),
-    ("gather2", 0), ("gather1", 3), ("far", 7), ("near", 7), ("near", 6), ("near", 5), ("mom", 5), ("gather1", 2),
-    ("forward2", 1), ("sum", 6), ("gather1", 4), ("sum", 7), ("forward2", 0), ("gather2", 3), ("sum", 5),
-    ("gather2", 2), ("gather1", 6), ("gather1", 7), ("gather1", 5), ("forward2", 3), ("gather2", 4), ("gather2", 6),
-    ("gather2", 5), ("sums", 0), ("gather2", 7), ("forward2", 2), ("forward2", 4), ("forward2", 5), ("forward2", 6),
-    ("norm", 0), ("forward2", 7), ("scale", 0), ("scale", 3), ("scale", 1), ("scale", 2), ("gram", 0), ("gram", 1),
+    ("dd", 0), ("dd", 4), ("dd", 6), ("far", 0), ("dd", 2), ("near", 0), ("dd", 3), ("dd", 1), ("far", 2), ("far", 1),
+    ("near", 2), ("sum", 0), ("dd", 5), ("near", 1), ("far", 3), ("sum", 1), ("sum", 2), ("near", 3), ("gather1", 0),
+    ("far", 4), ("dd", 7), ("sum", 3), ("far", 5), ("gather1", 1), ("near", 4), ("far", 6), ("gather1", 2),
+    ("sum", 4), ("far", 7), ("gather2", 0), ("gather1", 3), ("near", 5), ("sum", 5), ("near", 7), ("gather2", 1),
+    ("near", 6), ("sum", 6), ("gather2", 2), ("gather1", 4), ("sum", 7), ("forward2", 0), ("gather1", 5),
+    ("gather2", 3), ("gather1", 6), ("gather1", 7), ("forward2", 1), ("gather2", 4), ("gather2", 5), ("forward2", 2),
+    ("gather2", 6), ("sums", 0), ("gather2", 7), ("forward2", 3), ("forward2", 4), ("forward2", 5), ("forward2", 6),
+    ("forward2", 7), ("norm", 0), ("scale", 2), ("scale", 1), ("scale", 0), ("scale", 3), ("gram", 0), ("gram", 1),
     ("scale", 4), ("scale", 5), ("gram", 2), ("scale", 6), ("scale", 7), ("gram", 3),
 )
 
-CHUNK_GROUPS = ("dd0", "dd1", "p2", "p1", "mom", "g1", "g2", "f2")
-LATE_GROUPS = ("sqz", "sqy", "back", "w3", "w4", "fa", "fb", "fs", "s1", "q", "s2")
+CHUNK_GROUPS = ("dd0", "dd1", "p2", "p1", "g1", "g2", "f2")
+LATE_GROUPS = ("mom", "sqz", "sqy", "back", "w3", "w4", "fa", "fb", "fs", "s1", "q", "s2")
 SEND_GROUPS = ("dd", "rs", "mom", "back", "sq", "g1", "g2", "w3", "w4", "last")
 N_RECV = NC * len(CHUNK_GROUPS) + len(LATE_GROUPS)
 N_LOCAL = NC + 2
 
 
 def muon_kernel(grad, mom, weight, rate, decay, mom_out, weight_out, full_out,
-                own_g, sib_g, p2a, p1b, p1a, m2b, m1a, m1b, mom_x, mom_y, mom_r, gath, sq_own, sq_z, sq_y,
+                own_g, sib_g, p2a, p1b, p1a, m2b, m1a, m1b, mom_s, mix, mom_r, gath, sq_own, sq_z, sq_y,
                 x_cur, gram, poly, w_full, x_full, send_sems, recv_sems, local_sems):
     me = lax.axis_index("dp")
     tp = lax.axis_index("tp")
@@ -95,34 +95,43 @@
         for s in range(4):
             pltpu.make_async_copy(grad.at[slots[s] * 2 + core, :, pl.ds(r * RC, RC), :], own_g.at[s, r],
                                   local_sems.at[r]).start()
-        pltpu.make_async_copy(mom.at[me, pl.ds(r * RC, RC), :], mom_x.at[r, me], local_sems.at[NC]).start()
+    mom_load = pltpu.make_async_copy(mom, mom_out, local_sems.at[NC])
+    mom_load.start()
 
     with jax.named_scope("entry"):
         pl.semaphore_wait(barrier, 13)
-
-    def mom_(r):
-        for d in peers():
-            send(mom.at[d, pl.ds(r * RC, RC), :], mom_x.at[r, me], "mom", "mom", r, dp=d)
 
     def dd(r):
         for s in range(4):
             send(grad.at[slots[s] * 2 + 1 - core, :, pl.ds(r * RC, RC), :], sib_g.at[s, r], "dd", "dd1" if s else "dd0",
                  r, dp=sib)
+        if r == 0:
+            for s in range(4):
+                send(mom.at[slots[s] * 2 + 1 - core], mom_s.at[s], "mom", "mom", dp=sib)
 
     lo, hi = pl.ds(0, 4), pl.ds(4, 4)
+
+    def chip_terms(s, r):
+        rows = pl.ds(r * RC, RC)
+        own_g[s, r] = (own_g[s, r] + sib_g[s, r]) * (1.0 / 8.0)
+        own_g[s, r, me] = own_g[s, r, me] + MIX * mom_out[slots[s] * 2 + core, rows]
+        own_g[s, r, sib] = own_g[s, r, sib] + MIX * mom_s[s, rows]
 
     def far(r):
         drain(local_sems.at[r], own_g.at[:, r])
+        if r == 0:
+            mom_load.wait()
+            arrived(mom_s, "mom")
         arrived(sib_g.at[0, r], "dd0", r)
-        own_g[0, r] = own_g[0, r] + sib_g[0, r]
+        chip_terms(0, r)
         send(own_g.at[0, r, lo], p2a.at[r], "rs", "p2", r, dp=dp_xp)
         send(own_g.at[0, r, hi], m2b.at[r], "rs", "p2", r, dp=dp_xm)
 
     def near(r):
         arrived(sib_g.at[pl.ds(1, 3), r], "dd1", r)
-        own_g[1, r] = own_g[1, r] + sib_g[1, r]
+        chip_terms(1, r)
         send(own_g.at[1, r, hi], p1b.at[r], "rs", "p1", r, dp=dp_xp)
-        own_g[2, r] = own_g[2, r] + sib_g[2, r]
+        chip_terms(2, r)
         send(own_g.at[2, r, lo], m1a.at[r], "rs", "p1", r, dp=dp_xm)
 
     def sum_(r):
@@ -136,34 +145,37 @@
 
     def gather1(r):
         if not started:
-            drain(local_sems.at[NC], mom_x.at[:, 0])
             sq_own[...] = jnp.zeros_like(sq_own)
         started.append(r)
         arrived(own_g.at[pl.ds(0, 2), r], "p1", r)
-        arrived(mom_x.at[r, pl.ds(0, 7)], "mom", r)
+        chip_terms(3, r)
         for half, (near_ref, far_ref) in enumerate(((m1a, p1a), (p1b, m1b))):
             ds = pl.ds(half * 4, 4)
-            total = (own_g[3, r, ds] + sib_g[3, r, ds]) + (near_ref[r] + far_ref[r])
-            mean = total * (1.0 / 8.0)
-            mom_new = MOMENTUM * mom_x[r, ds] + mean
-            mom_y[ds, pl.ds(r * RC, RC)] = mom_new
-            upd = (mean + MOMENTUM * mom_new).astype(BF16)
+            total = own_g[3, r, ds] + (near_ref[r] + far_ref[r])
+            mix[ds, pl.ds(r * RC, RC)] = total
+            upd = ((1.0 + MOMENTUM) * total).astype(BF16)
             gath[z, y, r, ds] = upd
             upd = upd.astype(F32)
             sq_own[...] += jnp.sum((upd * upd).reshape(RC // 2, 8, 128), axis=0)
         for near_first in ((tp_zp, tp_yp), (tp_zm, tp_ym), (tp_z2, tp_y2)):
             send(gath.at[z, y, r, lo], gath.at[z, y, r, lo], "g1", "g1", r, tp=near_first[0])
             send(gath.at[z, y, r, hi], gath.at[z, y, r, hi], "g1", "g1", r, tp=near_first[1])
+        for t in (tp_yp, tp_ym):
+            send(gath.at[z, y, r, lo], gath.at[z, y, r, lo], "g2", "g2", r, tp=t)
+        for t in (tp_zp, tp_zm):
+            send(gath.at[z, y, r, hi], gath.at[z, y, r, hi], "g2", "g2", r, tp=t)
         if len(started) == NC:
             for t in (tp_zp, tp_zm, tp_z2):
                 send(sq_own, sq_z.at[z], "sq", "sqz", tp=t)
 
     def gather2(r):
         arrived(gath.at[0, pl.ds(0, 3), r], "g1", r)
-        for t in (tp_yp, tp_ym):
-            send(gath.at[:, y, r, lo], gath.at[:, y, r, lo], "g2", "g2", r, tp=t)
-        for t in (tp_zp, tp_zm):
-            send(gath.at[z, :, r, hi], gath.at[z, :, r, hi], "g2", "g2", r, tp=t)
+        for other in (zp, zm, z2):
+            for t in (tp_yp, tp_ym):
+                send(gath.at[other, y, r, lo], gath.at[other, y, r, lo], "g2", "g2", r, tp=t)
+        for other in (yp, ym, y2):
+            for t in (tp_zp, tp_zm):
+                send(gath.at[z, other, r, hi], gath.at[z, other, r, hi], "g2", "g2", r, tp=t)
 
     def forward2(r):
         arrived(gath.at[pl.ds(0, 2), :, r], "g2", r)
@@ -204,7 +216,7 @@
         if first + 256 < ROWS:
             dst[pl.ds(first, 256), pl.ds(first + 256, ROWS - first - 256)] = block[256:, :].T
 
-    stages = {"mom": mom_, "dd": dd, "far": far, "near": near, "sum": sum_, "gather1": gather1, "gather2": gather2,
+    stages = {"dd": dd, "far": far, "near": near, "sum": sum_, "gather1": gather1, "gather2": gather2,
               "forward2": forward2, "norm": norm, "scale": scale, "sums": sums, "gram": gram_rows}
     for name, r in ORDER:
         with jax.named_scope(f"{name}_{r}"):
@@ -217,7 +229,7 @@
     send(weight, w_full.at[:, me], "w4", "w4", dp=sib)
 
     for d in peers():
-        send(mom_y.at[d], mom_r.at[me], "back", "back", dp=d)
+        send(mix.at[d], mom_r.at[me], "back", "back", dp=d)
 
     def polynomial():
         for first in range(0, ROWS, 256):
@@ -276,13 +288,13 @@
         rows = pl.ds(pl.multiple_of(me * 128, 128), 128)
         weight_out[mat] = wo - lr * (OUT_SCALE * x_full[mat, rows].astype(F32) + dec * wo)
 
-    mom_r[me] = mom_y[me]
+    mom_r[me] = mix[me]
     arrived(mom_r.at[pl.ds(0, 7)], "back")
-    mom_out[...] = mom_r[...]
+    mom_out[...] = mom_r[...] + (MOMENTUM - MIX) * mom_out[...]
 
     pair = x_full.at[0]
     finish(me)
-    sent(("dd", own_g), ("rs", own_g.at[pl.ds(0, 3)]), ("mom", mom_x.at[:, pl.ds(0, 7)]),
+    sent(("dd", own_g), ("rs", own_g.at[pl.ds(0, 3)]), ("mom", mom_s),
          ("back", mom_r.at[pl.ds(0, 7)]), ("sq", mom_r.at[0, pl.ds(0, 48)]), ("g1", gath.at[0, pl.ds(0, 3)]),
          ("g2", gath.at[pl.ds(0, 3)]), ("w3", w_full.at[:, pl.ds(0, 3)]), ("w4", w_full.at[:, pl.ds(0, 4)]))
     arrived(pair, "fa")
@@ -327,7 +339,7 @@
                 V((4, NC, 8, RC, 128), F32), V((4, NC, 8, RC, 128), F32),
                 V((NC, 4, RC, 128), F32), V((NC, 4, RC, 128), F32), V((NC, 4, RC, 128), F32),
                 V((NC, 4, RC, 128), F32), V((NC, 4, RC, 128), F32), V((NC, 4, RC, 128), F32),
-                V((NC, 8, RC, 128), F32), V((8, 128, 128), F32), V((8, 128, 128), F32),
+                V((4, 128, 128), F32), V((8, 128, 128), F32), V((8, 128, 128), F32),
                 V((4, 4, NC, 8, RC, 128), BF16), V((8, 128), F32), V((4, 8, 128), F32), V((4, 8, 128), F32),
                 V((ROWS, COLS), BF16), V((ROWS, ROWS), BF16), V((ROWS, ROWS), BF16),
                 V((8, 8, 128, 128), F32), V((8, ROWS, 128), BF16),

time: 104 us -> 98.9 us (0.951)
  Pallas kernels: 99.2 us -> 94.6 us
    pallas_call x1, Pallas kernels: 99.2 us -> 94.6 us  [local_step(): pl.pallas_call(muon_kernel, out_shape=(V((8, 128, 128), F32), V((8, 128,...]
where the time goes in v5:
time: 98.9 us; the launch traced here: 98.8 us
  Pallas kernels  94.6 us (96%)
  local copies, waits for them, and re-layouts  2.91 us (3%)
  between operations  1.29 us (1%)
    pallas_call x1, Pallas kernels, local_step(): pl.pallas_call(muon_kernel, out_shape=(V((8, 128, 128), F32), V((8, 128,...  94.6 us
    unnamed x3, local copies, waits for them, and re-layouts  2.91 us

profile of v5, /device:TPU:1, one launch (start us, length us, event | category | flops | bytes accessed | tf_op | source)
XLA Modules:
  0.0 98.8 jit_solution(10922103748024854576)
XLA Ops:
  1.3 94.6 %muon_step.1 = (f32[8,128,128]{2,1,0:T(8,128)S(1)}, f32[8,128,128]{2,1,0:T(8,128)S(1)}, bf16[8,1024,128]{2,1,0:T(8,128)(2,1)S(1)}) custom-call(f32[8,8,128,128]{3,2,1,0:T(8,128)} %bitcast.3, f32[8,128,128]{2,1,0:T(8,128)} %mom.1, f32[8,128,128]{2,1,0:T(8,128)} %weight.1, f32[8]{0:T(128)} %rate.1, f32[1]{0:T(128)} %bitcast.2.decay), custom_call_target="tpu_custom_call" | custom-call | tf_op jit(solution)/shard_map/muon_step/pallas_call | solution.py:329
  95.9 0.8 copy.11
  96.7 0.8 copy.12
  97.5 1.3 %copy.13 = bf16[8,1024,128]{2,1,0:T(8,128)(2,1)} copy(bf16[8,1024,128]{2,1,0:T(8,128)(2,1)S(1)} %get-tuple-element.5) | data formatting | bytes 4194304

commit v6 on v5

--- a/solution.py
+++ b/solution.py
@@ -50,8 +50,8 @@
 N_LOCAL = NC + 2
 
 
-def muon_kernel(grad, mom, weight, rate, decay, mom_out, weight_out, full_out,
-                own_g, sib_g, p2a, p1b, p1a, m2b, m1a, m1b, mom_s, mix, mom_r, gath, sq_own, sq_z, sq_y,
+def muon_kernel(grad, mom, weight, rate, decay, pair_out, full_out,
+                own_g, sib_g, p2a, p1b, p1a, m2b, m1a, m1b, mom_v, mom_s, mix, mom_r, gath, sq_own, sq_z, sq_y,
                 x_cur, gram, poly, w_full, x_full, send_sems, recv_sems, local_sems):
     me = lax.axis_index("dp")
     tp = lax.axis_index("tp")
@@ -95,7 +95,7 @@
         for s in range(4):
             pltpu.make_async_copy(grad.at[slots[s] * 2 + core, :, pl.ds(r * RC, RC), :], own_g.at[s, r],
                                   local_sems.at[r]).start()
-    mom_load = pltpu.make_async_copy(mom, mom_out, local_sems.at[NC])
+    mom_load = pltpu.make_async_copy(mom, mom_v, local_sems.at[NC])
     mom_load.start()
 
     with jax.named_scope("entry"):
@@ -114,7 +114,7 @@
     def chip_terms(s, r):
         rows = pl.ds(r * RC, RC)
         own_g[s, r] = (own_g[s, r] + sib_g[s, r]) * (1.0 / 8.0)
-        own_g[s, r, me] = own_g[s, r, me] + MIX * mom_out[slots[s] * 2 + core, rows]
+        own_g[s, r, me] = own_g[s, r, me] + MIX * mom_v[slots[s] * 2 + core, rows]
         own_g[s, r, sib] = own_g[s, r, sib] + MIX * mom_s[s, rows]
 
     def far(r):
@@ -286,11 +286,11 @@
         full_out[mat] = new.astype(BF16)
         wo = w_full[mat, me]
         rows = pl.ds(pl.multiple_of(me * 128, 128), 128)
-        weight_out[mat] = wo - lr * (OUT_SCALE * x_full[mat, rows].astype(F32) + dec * wo)
+        pair_out[1, mat] = wo - lr * (OUT_SCALE * x_full[mat, rows].astype(F32) + dec * wo)
 
     mom_r[me] = mix[me]
     arrived(mom_r.at[pl.ds(0, 7)], "back")
-    mom_out[...] = mom_r[...] + (MOMENTUM - MIX) * mom_out[...]
+    pair_out[0] = mom_r[...] + (MOMENTUM - MIX) * mom_v[...]
 
     pair = x_full.at[0]
     finish(me)
@@ -326,20 +326,19 @@
         vmem = pl.BlockSpec(memory_space=pltpu.VMEM)
         smem = pl.BlockSpec(memory_space=pltpu.SMEM)
         V = pltpu.VMEM
-        return pl.pallas_call(
+        pair, weight_low = pl.pallas_call(
             muon_kernel,
             out_shape=(
-                V((8, 128, 128), F32),
-                V((8, 128, 128), F32),
+                V((2, 8, 128, 128), F32),
                 V((8, 1024, 128), BF16),
             ),
             in_specs=[hbm, hbm, hbm, smem, smem],
-            out_specs=(vmem, vmem, vmem),
+            out_specs=(vmem, vmem),
             scratch_shapes=[
                 V((4, NC, 8, RC, 128), F32), V((4, NC, 8, RC, 128), F32),
                 V((NC, 4, RC, 128), F32), V((NC, 4, RC, 128), F32), V((NC, 4, RC, 128), F32),
                 V((NC, 4, RC, 128), F32), V((NC, 4, RC, 128), F32), V((NC, 4, RC, 128), F32),
-                V((4, 128, 128), F32), V((8, 128, 128), F32), V((8, 128, 128), F32),
+                V((8, 128, 128), F32), V((4, 128, 128), F32), V((8, 128, 128), F32), V((8, 128, 128), F32),
                 V((4, 4, NC, 8, RC, 128), BF16), V((8, 128), F32), V((4, 8, 128), F32), V((4, 8, 128), F32),
                 V((ROWS, COLS), BF16), V((ROWS, ROWS), BF16), V((ROWS, ROWS), BF16),
                 V((8, 8, 128, 128), F32), V((8, ROWS, 128), BF16),
@@ -350,6 +349,7 @@
                 collective_id=0, has_side_effects=True, vmem_limit_bytes=63_400_000),
             name="muon_step",
         )(grad_local.reshape(8, 8, 128, 128), mom_local, weight_local, learn_rate, decay_rate.reshape(1))
+        return pair[0], pair[1], weight_low
 
     return jax.shard_map(
         local_step,

time: 98.9 us -> 98.4 us (level)
    unnamed x3 -> x1, local copies, waits for them, and re-layouts: 2.91 us -> 1.32 us
    squeeze x0 -> x1, local copies, waits for them, and re-layouts: none -> 1.06 us  [local_step(): return (pair[0], pair[1], weight_low)]
where the time goes in v6:
time: 98.4 us; the launch traced here: 98.2 us
  Pallas kernels  94.6 us (96%)
  local copies, waits for them, and re-layouts  2.38 us (2%)
  between operations  1.29 us (1%)
    pallas_call x1, Pallas kernels, local_step(): pl.pallas_call(muon_kernel, out_shape=(V((2, 8, 128, 128), F32), V((8, 10...  94.6 us

profile of v6, /device:TPU:1, one launch (start us, length us, event | category | flops | bytes accessed | tf_op | source)
XLA Modules:
  0.0 98.2 jit_solution(1421589493065292155)
XLA Ops:
  1.3 94.6 %muon_step.1 = (f32[2,8,128,128]{3,2,1,0:T(8,128)S(1)}, bf16[8,1024,128]{2,1,0:T(8,128)(2,1)S(1)}) custom-call(f32[8,8,128,128]{3,2,1,0:T(8,128)} %bitcast.7, f32[8,128,128]{2,1,0:T(8,128)} %mom.1, f32[8,128,128]{2,1,0:T(8,128)} %weight.1, f32[8]{0:T(128)} %rate.1, f32[1]{0:T(128)} %bitcast.6.decay), custom_call_target="tpu_custom_call" | custom-call | tf_op jit(solution)/shard_map/muon_step/pallas_call | solution.py:329
  95.9 1.1 %slice_bitcast_fusion = (f32[8,128,128]{2,1,0:T(8,128)}, f32[8,128,128]{2,1,0:T(8,128)}) fusion(f32[2,8,128,128]{3,2,1,0:T(8,128)S(1)} %get-tuple-element.5), kind=kLoop, calls=%fused_computation | loop fusion | bytes 2097152 | tf_op jit(solution)/shard_map/squeeze | solution.py:352
  96.9 1.3 %copy.9 = bf16[8,1024,128]{2,1,0:T(8,128)(2,1)} copy(bf16[8,1024,128]{2,1,0:T(8,128)(2,1)S(1)} %get-tuple-element.11) | data formatting | bytes 4194304

commit v7 on v6

--- a/solution.py
+++ b/solution.py
@@ -47,7 +47,7 @@
 LATE_GROUPS = ("mom", "sqz", "sqy", "back", "w3", "w4", "fa", "fb", "fs", "s1", "q", "s2")
 SEND_GROUPS = ("dd", "rs", "mom", "back", "sq", "g1", "g2", "w3", "w4", "last")
 N_RECV = NC * len(CHUNK_GROUPS) + len(LATE_GROUPS)
-N_LOCAL = NC + 2
+N_LOCAL = 4
 
 
 def muon_kernel(grad, mom, weight, rate, decay, pair_out, full_out,
@@ -94,8 +94,8 @@
     for r in range(NC):
         for s in range(4):
             pltpu.make_async_copy(grad.at[slots[s] * 2 + core, :, pl.ds(r * RC, RC), :], own_g.at[s, r],
-                                  local_sems.at[r]).start()
-    mom_load = pltpu.make_async_copy(mom, mom_v, local_sems.at[NC])
+                                  local_sems.at[min(r, 1)]).start()
+    mom_load = pltpu.make_async_copy(mom, mom_v, local_sems.at[2])
     mom_load.start()
 
     with jax.named_scope("entry"):
@@ -117,8 +117,14 @@
         own_g[s, r, me] = own_g[s, r, me] + MIX * mom_v[slots[s] * 2 + core, rows]
         own_g[s, r, sib] = own_g[s, r, sib] + MIX * mom_s[s, rows]
 
+    loaded = []
+
     def far(r):
-        drain(local_sems.at[r], own_g.at[:, r])
+        if r == 0:
+            drain(local_sems.at[0], own_g.at[:, 0])
+        elif not loaded:
+            drain(local_sems.at[1], own_g.at[:, pl.ds(1, NC - 1)])
+            loaded.append(r)
         if r == 0:
             mom_load.wait()
             arrived(mom_s, "mom")
@@ -222,7 +228,7 @@
         with jax.named_scope(f"{name}_{r}"):
             stages[name](r)
 
-    w_own = pltpu.make_async_copy(weight, w_full.at[:, me], local_sems.at[NC + 1])
+    w_own = pltpu.make_async_copy(weight, w_full.at[:, me], local_sems.at[3])
     w_own.start()
     for d in (dp_xp, dp_xm, dp_x2):
         send(weight, w_full.at[:, me], "w3", "w3", dp=d)

time: 98.4 us -> 98.3 us (level)
  no operation moved by 1% of the time
where the time goes in v7:
time: 98.3 us; the launch traced here: 98.2 us
  Pallas kernels  94.5 us (96%)
  local copies, waits for them, and re-layouts  2.38 us (2%)
  between operations  1.29 us (1%)
    pallas_call x1, Pallas kernels, local_step(): pl.pallas_call(muon_kernel, out_shape=(V((2, 8, 128, 128), F32), V((8, 10...  94.5 us

profile of v7, /device:TPU:1, one launch (start us, length us, event | category | flops | bytes accessed | tf_op | source)
XLA Modules:
  0.0 98.2 jit_solution(9286802703318580598)
XLA Ops:
  1.3 94.5 %muon_step.1 = (f32[2,8,128,128]{3,2,1,0:T(8,128)S(1)}, bf16[8,1024,128]{2,1,0:T(8,128)(2,1)S(1)}) custom-call(f32[8,8,128,128]{3,2,1,0:T(8,128)} %bitcast.7, f32[8,128,128]{2,1,0:T(8,128)} %mom.1, f32[8,128,128]{2,1,0:T(8,128)} %weight.1, f32[8]{0:T(128)} %rate.1, f32[1]{0:T(128)} %bitcast.6.decay), custom_call_target="tpu_custom_call" | custom-call | tf_op jit(solution)/shard_map/muon_step/pallas_call | solution.py:335
  95.8 1.1 %slice_bitcast_fusion = (f32[8,128,128]{2,1,0:T(8,128)}, f32[8,128,128]{2,1,0:T(8,128)}) fusion(f32[2,8,128,128]{3,2,1,0:T(8,128)S(1)} %get-tuple-element.5), kind=kLoop, calls=%fused_computation | loop fusion | bytes 2097152 | tf_op jit(solution)/shard_map/squeeze | solution.py:358
  96.9 1.3 %copy.9 = bf16[8,1024,128]{2,1,0:T(8,128)(2,1)} copy(bf16[8,1024,128]{2,1,0:T(8,128)(2,1)S(1)} %get-tuple-element.11) | data formatting | bytes 4194304
